TPU v7x, 256 devices: a whole 4x4x8 slice. The times are simulated.
256 devices in a mesh: dp: 32 (over z_lo, x, core), feat: 8 (over y, z_hi).
Axes of the slice: x: 4, y: 4, z: 8 (z_hi: 2, z_lo: 4; z = z_hi * 4 + z_lo), core: 2. Of those that a mesh axis runs over, the one named last changes fastest.
Arguments:
- view_a: bfloat16 [4096, 4096], P('dp', 'feat'), may hold values from -24 to 24
- view_b: bfloat16 [4096, 4096], P('dp', 'feat'), may hold values from -24 to 24
Outputs:
- grad_a: bfloat16 [4096, 4096], P('dp', 'feat')
- grad_b: bfloat16 [4096, 4096], P('dp', 'feat')
- loss: float32 [], replicated
All inputs are finite; a program needn't handle non-finite values.
Results may differ from a plain program's by a relative error of at most 0.0068.
Values may be sent and summed in bfloat16 or wider, within the bound.
A program may use at most 64 MiB of HBM per device.

v0:
```python
import jax
import jax.numpy as jnp
from jax import lax
from jax.sharding import Mesh
from jax.sharding import PartitionSpec as P

F = 4096
DP = ("dp_0", "dp_1", "dp_2")
FEAT = ("feat_0", "feat_1")
DP_FEAT = ("dp_0", "dp_1", "dp_2", "feat_0", "feat_1")


EPS = 1e-05
LAMBDA = 0.0051


def from_everyone(x, axis):
    copies = jnp.broadcast_to(x, (lax.axis_size(axis), *x.shape))
    return lax.all_to_all(copies, axis, split_axis=0, concat_axis=0, tiled=True)


def of_everyone(x, axis):
    return from_everyone(x, axis).sum(axis=0)


def in_one(arrays, axis):
    line, at, gathered = (jnp.concatenate([a.reshape(-1) for a in arrays]), 0, [])
    running = of_everyone(line, axis)
    for a in arrays:
        gathered.append(running[at : at + a.size].reshape(a.shape))
        at += a.size
    return tuple(gathered)


def joined_along(parts, dim):
    parts = jnp.moveaxis(parts, 0, dim)
    dims = parts.shape
    return parts.reshape(*dims[:dim], dims[dim] * dims[dim + 1], *dims[dim + 2 :])


def collect(x, axis, dim):
    parts = from_everyone(x, axis)
    return joined_along(parts, dim)


def split_up(x, dim, length):
    before, after = (x.shape[:dim], x.shape[dim + 1 :])
    return jnp.moveaxis(x.reshape(*before, length, -1, *after), dim, 0)


def scatter_pairs(x, chips, core, dim):
    sizes = (lax.axis_size(chips), lax.axis_size(core))
    parts = split_up(x, dim, sizes[0] * sizes[1])
    inside = parts.shape[1:]
    parts = parts.reshape(*sizes, *inside).swapaxes(0, 1).reshape(-1, *inside)
    parts = lax.psum_scatter(parts, core, scatter_dimension=0, tiled=True)
    return lax.psum_scatter(parts, chips, scatter_dimension=0, tiled=True)[0]


def over_axes(x, axes):
    for axis in axes:
        x = lax.psum(x, axis)
    return x


def shards(view_a, view_b):
    rows, local = view_a.shape
    groups = lax.axis_size(DP)
    count = rows * groups
    vals_a = view_a.astype(jnp.float32)
    vals_b = view_b.astype(jnp.float32)
    sums = in_one(
        (
            jnp.sum(vals_a, axis=0),
            jnp.sum(vals_a * vals_a, axis=0),
            jnp.sum(vals_b, axis=0),
            jnp.sum(vals_b * vals_b, axis=0),
        ),
        DP,
    )
    center_a = sums[0] / count
    center_b = sums[2] / count
    inverse_a = lax.rsqrt(sums[1] / count - center_a * center_a + EPS)
    inverse_b = lax.rsqrt(sums[3] / count - center_b * center_b + EPS)
    normed_a = (vals_a - center_a) * inverse_a
    normed_b = (vals_b - center_b) * inverse_b
    a_half = normed_a.astype(jnp.bfloat16)
    b_half = normed_b.astype(jnp.bfloat16)
    b_every = collect(b_half, FEAT, 1)
    block_rows = F // groups
    corr_t = (
        scatter_pairs(
            lax.dot_general(
                b_every, a_half, (((0,), (0,)), ((), ())), preferred_element_type=jnp.float32
            ),
            ("dp_0", "dp_1"),
            "dp_2",
            0,
        )
        / count
    )
    row_ids = lax.axis_index(DP) * block_rows + lax.broadcasted_iota(
        jnp.int32, (block_rows, local), 0
    )
    col_ids = lax.axis_index(FEAT) * local + lax.broadcasted_iota(jnp.int32, (block_rows, local), 1)
    unit = (row_ids == col_ids).astype(jnp.float32)
    partial_loss = jnp.sum(unit * (1.0 - corr_t) ** 2) + LAMBDA * jnp.sum(
        (1.0 - unit) * corr_t * corr_t
    )
    loss = over_axes(partial_loss, DP_FEAT) / F
    grad_t = (unit * (-2.0 * (1.0 - corr_t)) + (1.0 - unit) * (2.0 * LAMBDA) * corr_t).astype(
        jnp.bfloat16
    )
    grad_full = lax.all_gather(grad_t, DP, axis=0, tiled=True)
    grad_na = jnp.dot(b_every, grad_full, preferred_element_type=jnp.float32)
    partial_b = lax.dot_general(
        a_half, grad_full, (((1,), (1,)), ((), ())), preferred_element_type=jnp.float32
    )
    grad_nb = lax.psum_scatter(partial_b, FEAT, scatter_dimension=1, tiled=True)
    stats = in_one(
        (
            jnp.sum(grad_na, axis=0),
            jnp.sum(grad_na * normed_a, axis=0),
            jnp.sum(grad_nb, axis=0),
            jnp.sum(grad_nb * normed_b, axis=0),
        ),
        DP,
    )
    grad_a = (inverse_a * (grad_na - stats[0] / count - normed_a * (stats[1] / count))).astype(
        jnp.bfloat16
    )
    grad_b = (inverse_b * (grad_nb - stats[2] / count - normed_b * (stats[3] / count))).astype(
        jnp.bfloat16
    )
    return (grad_a, grad_b, loss)


def solution(mesh):
    torus = Mesh(mesh.devices.reshape(4, 4, 2, 4, 2), ("dp_0", "dp_1", "dp_2", "feat_0", "feat_1"))
    in_specs = (P(DP, FEAT), P(DP, FEAT))
    out_specs = (P(DP, FEAT), P(DP, FEAT), P())
    return jax.shard_map(
        shards, mesh=torus, in_specs=in_specs, out_specs=out_specs, check_vma=False
    )
```

profile of v0, /device:TPU:1, one launch (start us, length us, event | category | flops | bytes accessed | tf_op | source)
XLA Modules:
  0.0 412.4 jit_solution(12478503057353456559)
XLA Ops:
  7.2 0.0 copy-start
  7.2 0.0 reduce-scatter.4.cloned.1.call-start
  7.2 1.1 convert_reduce_fusion
  8.3 0.1 broadcast_in_dim.6
  8.5 20.9 %all_to_all.17 = f32[32,1,2048]{2,1,0:T(1,128)S(1)} all-to-all(f32[32,1,2048]{2,1,0:T(1,128)S(1)} %broadcast_in_dim.6), channel_id=1, replica_groups=mesh['dp_0'=4,'dp_1'=4,'dp_2'=2,'feat_0'=4,'feat_1'=2] {'dp_0','dp_1','d..., dimensions={0} | all-to-all | bytes 524288 | tf_op jit(solution)/shard_map/all_to_all | solution.py:19
  29.4 0.2 reduce_sum.112
  29.5 0.9 fusion.13
  30.5 0.1 copy.11
  30.6 0.1 broadcast_in_dim.7
  30.7 32.7 %all_to_all.18 = bf16[8,128,512]{1,2,0:T(8,128)(2,1)S(1)} all-to-all(bf16[8,128,512]{1,2,0:T(8,128)(2,1)S(1)} %broadcast_in_dim.7), channel_id=1, replica_groups=mesh['dp_0'=4,'dp_1'=4,'dp_2'=2,'feat_0'=4,'feat_1'=2] {'feat_0','feat_1'}, dimensions={0} | all-to-all | bytes 2097152 | tf_op jit(solution)/shard_map/all_to_all | solution.py:19
  63.4 0.0 copy-done
  63.4 1.3 convolution_bitcast_fusion
  64.7 4.2 %copy.12 = f32[2,16,128,512]{3,2,1,0:T(8,128)} copy(f32[2,16,128,512]{3,2,0,1:T(8,128)S(1)} %convolution_bitcast_fusion) | data formatting | bytes 16777216 | tf_op jit(solution)/shard_map/transpose | solution.py:55
  68.9 0.0 reduce-scatter.4.cloned.1.call-update
  69.0 0.0 reduce-scatter.6.cloned.1.call-start
  69.0 21.2 %reduce-scatter.4.cloned.1.call-done = f32[16,128,512]{2,1,0:T(8,128)} async-done(((f32[32,128,512]{2,1,0:T(8,128)}), f32[16,128,512]{2,1,0:T(8,128)}) %reduce-scatter.4.cloned.1.call-update) | async-done | bytes 4194320 | tf_op jit(solution)/shard_map/reduce_scatter | solution.py:56
  90.2 0.0 reduce-scatter.6.cloned.1.call-update
  90.2 0.0 all-gather.2.cloned.1.call-start
  90.3 88.0 %reduce-scatter.6.cloned.1.call-done = f32[1,128,512]{2,1,0:T(8,128)} async-done(((f32[16,128,512]{2,1,0:T(8,128)}), f32[1,128,512]{2,1,0:T(8,128)}) %reduce-scatter.6.cloned.1.call-update) | async-done | bytes 262160 | tf_op jit(solution)/shard_map/reduce_scatter | solution.py:57
  178.3 2.4 fusion.18
  180.7 0.0 all-gather.2.cloned.1.call-update
  180.8 0.0 reduce-scatter.8.cloned.1.call-start
  180.8 69.2 %all-gather.2.cloned.1.call-done = bf16[4096,512]{1,0:T(8,128)(2,1)} async-done(((bf16[128,512]{1,0:T(8,128)(2,1)}), bf16[4096,512]{1,0:T(8,128)(2,1)}) %all-gather.2.cloned.1.call-update) | async-done | bytes 4194320 | tf_op jit(solution)/shard_map/all_gather | solution.py:114
  250.0 5.0 %fusion.26 = f32[128,4096]{1,0:T(8,128)} fusion(bf16[4096,512]{1,0:T(8,128)(2,1)} %all-gather.2.cloned.1.call-done, bf16[128,512]{1,0:T(8,128)(2,1)S(1)} %copy-done, f32[512]{0:T(512)S(1)} %get-tuple-element.20, f32[512]{0:T(512)S(1)} %get-tuple-element.18), kind=kOutput, calls=%fused_computation.38 | convolution fusion | flops 537133056 | bytes 6426624 | tf_op jit(solution)/shard_map/dot_general | solution.py:116
  255.0 0.0 copy-start.1
  255.0 0.0 reduce-scatter.8.cloned.1.call-update
  255.1 3.0 fusion.35
  258.1 89.4 %reduce-scatter.8.cloned.1.call-done = f32[128,512]{1,0:T(8,128)} async-done(((f32[128,4096]{1,0:T(8,128)}), f32[128,512]{1,0:T(8,128)}) %reduce-scatter.8.cloned.1.call-update) | async-done | bytes 262160 | tf_op jit(solution)/shard_map/reduce_scatter | solution.py:119
  347.5 0.0 copy-done.1
  347.5 1.0 fusion.36
  348.5 0.8 broadcast_in_dim.8
  349.3 7.3 %all-to-all-start.2 = ((f32[32,1,2048]{2,1,0:T(1,128)}), f32[32,1,2048]{2,1,0:T(1,128)S(1)}, u32[]{:S(2)}, u32[]{:S(2)}) async-start(f32[32,1,2048]{2,1,0:T(1,128)} %broadcast_in_dim.8), calls=%async_computation.5 | async-start | bytes 524288 | tf_op jit(solution)/shard_map/all_to_all | solution.py:19
  358.0 10.6 %psum.35 = f32[]{:T(128)} all-reduce(f32[]{:T(128)S(6)} %add.61), channel_id=1, replica_groups=mesh['dp_0'=4,'dp_1'=4,'dp_2'=2,'feat_0'=4,'feat_1'=2] {'dp_0'}, use_global_device_ids=true, to_apply=%region_15.0 | all-reduce | flops 1 | bytes 8 | tf_op jit(solution)/shard_map/psum | solution.py:62
  368.6 8.9 %psum.36 = f32[]{:T(128)} all-reduce(f32[]{:T(128)} %psum.35), channel_id=1, replica_groups=mesh['dp_0'=4,'dp_1'=4,'dp_2'=2,'feat_0'=4,'feat_1'=2] {'dp_1'}, use_global_device_ids=true, to_apply=%region_16.0 | all-reduce | flops 1 | bytes 8 | tf_op jit(solution)/shard_map/psum | solution.py:62
  377.5 7.0 %psum.37 = f32[]{:T(128)} all-reduce(f32[]{:T(128)} %psum.36), channel_id=1, replica_groups=mesh['dp_0'=4,'dp_1'=4,'dp_2'=2,'feat_0'=4,'feat_1'=2] {'dp_2'}, use_global_device_ids=true, to_apply=%region_17.0 | all-reduce | flops 1 | bytes 8 | tf_op jit(solution)/shard_map/psum | solution.py:62
  384.5 8.7 %psum.38 = f32[]{:T(128)} all-reduce(f32[]{:T(128)} %psum.37), channel_id=1, replica_groups=mesh['dp_0'=4,'dp_1'=4,'dp_2'=2,'feat_0'=4,'feat_1'=2] {'feat_0'}, use_global_device_ids=true, to_apply=%region_18.0 | all-reduce | flops 1 | bytes 8 | tf_op jit(solution)/shard_map/psum | solution.py:62
  393.2 8.3 %psum.39 = f32[]{:T(128)} all-reduce(f32[]{:T(128)} %psum.38), channel_id=1, replica_groups=mesh['dp_0'=4,'dp_1'=4,'dp_2'=2,'feat_0'=4,'feat_1'=2] {'feat_1'}, use_global_device_ids=true, to_apply=%region_19.0 | all-reduce | flops 1 | bytes 8 | tf_op jit(solution)/shard_map/psum | solution.py:62
  402.2 0.0 all-to-all-done.2
  402.2 0.2 reduce_sum.117
  402.3 0.7 fusion.8
  403.1 1.7 fusion.17
  (6 shorter events, 0.0 us)
Async XLA Ops:
  7.2 56.3 %copy-start = (bf16[128,512]{1,0:T(8,128)(2,1)S(1)}, bf16[128,512]{1,0:T(8,128)(2,1)}, u32[]{:S(2)}) copy-start(bf16[128,512]{1,0:T(8,128)(2,1)} %param.2) | copy-start | bytes 393220
  7.2 83.0 %reduce-scatter.4.cloned.1.call-start = ((), (), s32[]{:S(2)}) async-start(), calls=%async_computation.6 | async-start | bytes 12582912 | tf_op jit(solution)/shard_map/reduce_scatter | solution.py:56
  69.0 109.3 %reduce-scatter.6.cloned.1.call-start = ((), (), s32[]{:S(2)}) async-start(), calls=%async_computation.7 | async-start | bytes 4456448 | tf_op jit(solution)/shard_map/reduce_scatter | solution.py:57
  90.2 159.8 %all-gather.2.cloned.1.call-start = ((), (), s32[]{:S(2)}) async-start(), calls=%async_computation.8 | async-start | bytes 4325376 | tf_op jit(solution)/shard_map/all_gather | solution.py:114
  180.8 166.7 %reduce-scatter.8.cloned.1.call-start = ((), (), s32[]{:S(2)}) async-start(), calls=%async_computation.9 | async-start | bytes 2359296 | tf_op jit(solution)/shard_map/reduce_scatter | solution.py:119
  255.0 92.4 %copy-start.1 = (bf16[128,512]{1,0:T(8,128)(2,1)S(1)}, bf16[128,512]{1,0:T(8,128)(2,1)}, u32[]{:S(2)}) copy-start(bf16[128,512]{1,0:T(8,128)(2,1)} %param.3) | copy-start | bytes 393220
  349.3 52.8 %all-to-all-start.2 = ((f32[32,1,2048]{2,1,0:T(1,128)}), f32[32,1,2048]{2,1,0:T(1,128)S(1)}, u32[]{:S(2)}, u32[]{:S(2)}) async-start(f32[32,1,2048]{2,1,0:T(1,128)} %broadcast_in_dim.8), calls=%async_computation.5 | async-start | bytes 524288 | tf_op jit(solution)/shard_map/all_to_all | solution.py:19
Sparse Core Ops, SparseCore 0:
  69.1 21.0 reduce-scatter.3
  92.8 85.4 reduce-scatter.5
  180.9 69.1 all-gather.1
  255.2 92.2 reduce-scatter.7
where the time goes:
time: 413 us; the launch traced here: 412 us
  waiting for transfers between devices  268 us (65%)
  blocking collectives  97.1 us (24%)
  between operations  17 us (4%)
  matrix products  9.24 us (2%)
  other arithmetic  8.25 us (2%)
  starting transfers between devices  7.48 us (2%)
  local copies, waits for them, and re-layouts  5.46 us (1%)
    reduce_scatter x1, waiting for transfers between devices, shards(): grad_nb = lax.psum_scatter(partial_b, FEAT, scatter_dimension=1, tiled=True)  89.4 us
    reduce_scatter x1, waiting for transfers between devices, scatter_pairs(): return lax.psum_scatter(parts, chips, scatter_dimension=0, tiled=True)[0]  88 us
    all_gather x1, waiting for transfers between devices, shards(): grad_full = lax.all_gather(grad_t, DP, axis=0, tiled=True)  69.2 us
    all_to_all x2, blocking collectives, from_everyone(): return lax.all_to_all(copies, axis, split_axis=0, concat_axis=0, tiled=True)  53.6 us
    psum x5, blocking collectives, over_axes(): x = lax.psum(x, axis)  43.5 us
    reduce_scatter x1, waiting for transfers between devices, scatter_pairs(): parts = lax.psum_scatter(parts, core, scatter_dimension=0, tiled=True)  21.2 us
  transfers between devices with their start and end apart: 5, of which 4 were waited for; matrix products, arithmetic and copies ran while one was open for 1% of the time, Pallas kernels for 0%

commit v1 on v0

v1 whole, which is shorter than its diff:
```python
import jax
import jax.numpy as jnp
from jax import lax
from jax.experimental import pallas as pl
from jax.experimental.pallas import tpu as pltpu
from jax.sharding import PartitionSpec as P

F = 4096
S = 4096
EPS = 1e-05
LAMBDA = 0.0051
MESH = pl.DeviceIdType.MESH
BF = jnp.bfloat16
F32 = jnp.float32


class Slots:
    def __init__(self):
        self.used = 0

    def take(self, n):
        first = self.used
        self.used += n
        return first


SEM = Slots()
I_V0 = SEM.take(1)
I_VZ = SEM.take(3)
I_XP, I_XM, I_XPF, I_XMF = (SEM.take(4) for _ in range(4))
I_W1 = SEM.take(2)
I_YP, I_YM, I_YPF, I_YMF = (SEM.take(2) for _ in range(4))
I_WD = SEM.take(8)
I_DA, I_DB, I_DZ = (SEM.take(1) for _ in range(3))
I_DY = SEM.take(3)
I_P1P, I_P1M = (SEM.take(4) for _ in range(2))
I_P2P, I_P2M = (SEM.take(8) for _ in range(2))
I_OZ = SEM.take(3)
I_OD = SEM.take(1)
I_GD = SEM.take(4)
I_Y1P, I_Y1M = (SEM.take(2) for _ in range(2))
I_Y2P, I_Y2M = (SEM.take(4) for _ in range(2))
I_A2 = SEM.take(2)
N_SEM = SEM.used


def kernel(
    a_in, b_in, ga_out, gb_out, loss_out,
    va, vbt, bt_loc, asum, asq, bsum, bsq, raw, g1, g2, rowv, colv,
    dtile, darr, dsum, dboth, ltile, lz, lzsum, ly,
    p1p_s, p1m_s, p1p_r, p1m_r, aug, p2p_s, p2m_s, p2p_r, p2m_r, ga_own,
    oz_s, oz_r, od_s, gfa,
    gd_s, gd_r, gb_own, y1p_s, y1m_s, y1p_r, y1m_r, y2p_s, y2m_s, y2p_r, y2m_r,
    a2_s, gfin, ssem, rsem,
):
    dp = lax.axis_index("dp")
    ft = lax.axis_index("feat")
    r, k = lax.div(dp, 2), lax.rem(dp, 2)
    zl, x = lax.div(r, 4), lax.rem(r, 4)
    y, zh = lax.div(ft, 2), lax.rem(ft, 2)
    o = 1 - k
    xp, x2, xm = lax.rem(x + 1, 4), lax.rem(x + 2, 4), lax.rem(x + 3, 4)
    yp, y2, ym = lax.rem(y + 1, 4), lax.rem(y + 2, 4), lax.rem(y + 3, 4)
    zq = (zl, zl + 1 - 2 * lax.rem(zl, 2), lax.rem(zl + 2, 4), 3 - zl)
    zhs = (zh, 1 - zh)

    def dev(r_, k_, f_):
        return (r_ * 2 + k_, f_)

    def rc(src, dst, i, to):
        return pltpu.make_async_remote_copy(
            src_ref=src, dst_ref=dst, send_sem=ssem.at[i], recv_sem=rsem.at[i],
            device_id=to, device_id_type=MESH,
        )

    def lanes(i, n):
        return pl.ds(pl.multiple_of(i * n, n), n)

    to_xp, to_xm = dev(zl * 4 + xp, k, ft), dev(zl * 4 + xm, k, ft)
    to_yp, to_ym = dev(r, k, yp * 2 + zh), dev(r, k, ym * 2 + zh)
    partner = dev(r, o, ft)

    barrier = pltpu.get_barrier_semaphore()

    def greet(to):
        pl.semaphore_signal(barrier, inc=1, device_id=to, device_id_type=MESH)

    greet(partner)
    for f_ in (yp, y2, ym):
        greet(dev(r, k, f_ * 2 + zh))

    @pl.loop(1, 16)
    def _(t):
        greet(dev(lax.rem(r + t, 16), k, ft))

    @pl.loop(0, 16)
    def _(t):
        greet(dev(lax.rem(r + t, 16), k, y * 2 + zhs[1]))

    for c in range(4):
        bt_loc[c * 128:(c + 1) * 128, :] = (
            b_in[:, c * 128:(c + 1) * 128].astype(F32).T.astype(BF)
        )
    va[k, r] = a_in[:, lanes(k, 256)]
    vbt[k, ft, :, lanes(r, 128)] = bt_loc[lanes(r, 32), :]
    pl.semaphore_wait(barrier, 35)

    c_v0 = rc(a_in.at[:, lanes(o, 256)], va.at[k, r], I_V0, partner)
    c_v0.start()

    def c_w1(t, h):
        to = lax.rem(r + t, 16)
        return rc(
            bt_loc.at[lanes(to, 32), :], vbt.at[k, ft, :, lanes(r, 128)],
            I_W1 + h, dev(to, k, y * 2 + zhs[h]),
        )

    @pl.loop(0, 16)
    def _(t):
        c_w1(t, 1).start()

    @pl.loop(1, 16)
    def _(t):
        c_w1(t, 0).start()

    w1_all = (
        rc(vbt.at[k, ft, :, 0:1920], vbt.at[k, ft, :, 0:1920], I_W1, partner),
        rc(vbt.at[k, y * 2 + zhs[1]], vbt.at[k, y * 2 + zhs[1]], I_W1 + 1, partner),
    )

    def c_vz(q):
        return rc(va.at[:, r], va.at[:, r], I_VZ + q - 1, dev(zq[q] * 4 + x, k, ft))

    def c_xp(q):
        s = zq[q] * 4 + x
        return rc(va.at[:, s], va.at[:, s], I_XP + q, to_xp)

    def c_xm(q):
        s = zq[q] * 4 + x
        return rc(va.at[:, s], va.at[:, s], I_XM + q, to_xm)

    def c_xpf(q):
        s = zq[q] * 4 + xm
        return rc(va.at[0, s], va.at[0, s], I_XPF + q, to_xp)

    def c_xmf(q):
        s = zq[q] * 4 + xp
        return rc(va.at[1, s], va.at[1, s], I_XMF + q, to_xm)

    def c_yp(h):
        s = y * 2 + zhs[h]
        return rc(vbt.at[k, s], vbt.at[k, s], I_YP + h, to_yp)

    def c_ym(h):
        s = y * 2 + zhs[h]
        return rc(vbt.at[k, s], vbt.at[k, s], I_YM + h, to_ym)

    def c_ypf(h):
        s = ym * 2 + zhs[h]
        return rc(vbt.at[k, s, 0:16], vbt.at[k, s, 0:16], I_YPF + h, to_yp)

    def c_ymf(h):
        s = yp * 2 + zhs[h]
        return rc(vbt.at[k, s, 16:32], vbt.at[k, s, 16:32], I_YMF + h, to_ym)

    def c_wd(j, h):
        s = (y, ym, yp, y2)[j] * 2 + zhs[h]
        return rc(vbt.at[k, s], vbt.at[k, s], I_WD + j * 2 + h, partner)

    c_v0.wait_recv()
    c_xp(0).start()
    c_xm(0).start()
    for q in (1, 2, 3):
        c_vz(q).start()
    for h in (0, 1):
        w1_all[h].wait_recv()
        c_yp(h).start()
        c_ym(h).start()
        c_wd(0, h).start()

    def x_next(q):
        c_vz(q).wait_recv()
        c_xp(q).start()
        c_xm(q).start()

    def x_forward(q):
        c_xp(q).wait_recv()
        c_xpf(q).start()
        c_xm(q).wait_recv()
        c_xmf(q).start()

    def y_forward(h):
        c_yp(h).wait_recv()
        c_ypf(h).start()
        c_wd(1, h).start()
        c_ym(h).wait_recv()
        c_ymf(h).start()
        c_wd(2, h).start()

    def y_last(h):
        c_ypf(h).wait_recv()
        c_ymf(h).wait_recv()
        c_wd(3, h).start()

    x_next(1)
    x_forward(0)
    y_forward(0)
    x_next(2)
    x_forward(1)
    y_forward(1)
    x_next(3)
    x_forward(2)
    y_last(0)
    x_forward(3)
    y_last(1)
    for q in range(4):
        c_xpf(q).wait_recv()
        c_xmf(q).wait_recv()
    for h in (0, 1):
        for j in range(4):
            c_wd(j, h).wait_recv()

    asum[...] = jnp.zeros_like(asum)
    asq[...] = jnp.zeros_like(asq)
    bsum[...] = jnp.zeros_like(bsum)
    bsq[...] = jnp.zeros_like(bsq)

    for kk in range(2):
        @pl.loop(0, 16)
        def _(c):
            blk = va[kk, c].astype(F32).reshape(16, 8, 256)
            asum[...] += jnp.sum(blk, axis=0)
            asq[...] += jnp.sum(blk * blk, axis=0)
            bl = vbt[kk, :, :, lanes(c, 128)].astype(F32).reshape(256, 128)
            bsum[...] += bl
            bsq[...] += bl * bl

    raw[...] = jnp.zeros_like(raw)
    for kk in range(2):
        @pl.loop(0, 4)
        def _(c):
            raw[...] += jnp.dot(
                vbt[kk, :, :, lanes(c, 512)].reshape(256, 512),
                va[kk, pl.ds(c * 4, 4)].reshape(512, 256),
                preferred_element_type=F32,
            )

    ma = jnp.sum(asum[...], axis=0, keepdims=True) / S
    inva = lax.rsqrt(jnp.sum(asq[...], axis=0, keepdims=True) / S - ma * ma + EPS)
    mb = jnp.sum(bsum[...], axis=1, keepdims=True) / S
    invb = lax.rsqrt(jnp.sum(bsq[...], axis=1, keepdims=True) / S - mb * mb + EPS)
    ct = (raw[...] / S - mb * ma) * (invb * inva)
    row = lax.broadcasted_iota(jnp.int32, (256, 256), 0)
    col = lax.broadcasted_iota(jnp.int32, (256, 256), 1)
    jrow = lax.shift_right_logical(row, 5) * 512 + lax.bitwise_and(row, 31) + r * 32
    unit = jrow == col + (ft * 512 + k * 256)
    zero = jnp.zeros_like(ct)
    g = jnp.where(unit, zero, (2.0 * LAMBDA) * ct)
    g1v = (invb * g).astype(BF)
    g2v = (g * inva).astype(BF)
    g1[...] = g1v
    g2[...] = g2v
    gc = g * ct
    ua = inva * jnp.sum(gc, axis=0, keepdims=True)
    ub = invb * jnp.sum(gc, axis=1, keepdims=True)
    rowv[0:1, :] = ua
    rowv[1:2, :] = jnp.sum(g1v.astype(F32) * mb, axis=0, keepdims=True) - ma * ua
    colv[:, 0:1] = ub
    colv[:, 1:2] = jnp.sum(g2v.astype(F32) * ma, axis=1, keepdims=True) - mb * ub

    def on_diag(v):
        return jnp.sum(jnp.where(unit, v, zero), axis=0, keepdims=True)

    dtile[...] = jnp.zeros_like(dtile)
    dtile[0:1, :] = on_diag(jnp.broadcast_to(ma, ct.shape))
    dtile[1:2, :] = on_diag(jnp.broadcast_to(inva, ct.shape))
    dtile[2:3, :] = on_diag(jnp.broadcast_to(mb, ct.shape))
    dtile[3:4, :] = on_diag(jnp.broadcast_to(invb, ct.shape))
    dtile[4:5, :] = on_diag(ct)
    dtile[5:6, :] = jnp.sum(
        jnp.where(unit, (1.0 - ct) * (1.0 - ct), LAMBDA * ct * ct), axis=0, keepdims=True
    )

    def c_da(t):
        return rc(dtile, darr.at[r], I_DA, dev(lax.rem(r + t, 16), k, ft))

    def ga_block(kk, s):
        prod = lax.dot_general(
            vbt[kk, :, :, lanes(s, 128)].reshape(256, 128), g1[...],
            (((0,), (0,)), ((), ())), preferred_element_type=F32,
        )
        return prod - va[kk, s].astype(F32) * rowv[0:1, :] - rowv[1:2, :]

    def gb_block(kk, c):
        prod = lax.dot_general(
            g2[...], va[kk, pl.ds(c * 2, 2)].reshape(256, 256),
            (((1,), (1,)), ((), ())), preferred_element_type=F32,
        )
        bl = vbt[kk, :, :, lanes(c, 256)].reshape(256, 256).astype(F32)
        return (prod - bl * colv[:, 0:1] - colv[:, 1:2]).reshape(8, 32, 256)

    def c_p1p(z):
        return rc(p1p_s.at[z], p1p_r.at[z], I_P1P + z, to_xp)

    def c_p1m(z):
        return rc(p1m_s.at[z], p1m_r.at[z], I_P1M + z, to_xm)

    def c_p2p(z, h):
        return rc(p2p_s.at[z, h], p2p_r.at[z, h], I_P2P + z * 2 + h, to_xp)

    def c_p2m(z, h):
        return rc(p2m_s.at[z, h], p2m_r.at[z, h], I_P2M + z * 2 + h, to_xm)

    @pl.loop(0, 4)
    def _(z):
        s = z * 4 + x2
        p1p_s[z] = ga_block(0, s).astype(BF)
        c_p1p(z).start()
        p1m_s[z] = ga_block(1, s).astype(BF)
        c_p1m(z).start()

    darr[r] = dtile[...]

    @pl.loop(1, 16)
    def _(t):
        c_da(t).start()

    def c_gd(c):
        at = lanes(c, 512)
        return rc(gd_s.at[:, :, at], gd_r.at[:, :, at], I_GD + c, partner)

    @pl.loop(0, 4)
    def _(c):
        for e in range(2):
            gd_s[:, :, lanes(c * 2 + e, 256)] = gb_block(o, c * 2 + e).astype(BF)
        c_gd(c).start()

    @pl.loop(0, 4)
    def _(z):
        p2p_s[z, 1] = ga_block(1, z * 4 + xp).astype(BF)
        c_p2p(z, 1).start()
        p2m_s[z, 0] = ga_block(0, z * 4 + xm).astype(BF)
        c_p2m(z, 0).start()

    @pl.loop(0, 4)
    def _(z):
        aug[0, z] = ga_block(0, z * 4 + xp)
        aug[1, z] = ga_block(1, z * 4 + xm)

    @pl.loop(0, 4)
    def _(z):
        c_p1p(z).wait_recv()
        p2p_s[z, 0] = (aug[0, z] + p1p_r[z].astype(F32)).astype(BF)
        c_p2p(z, 0).start()
        c_p1m(z).wait_recv()
        p2m_s[z, 1] = (aug[1, z] + p1m_r[z].astype(F32)).astype(BF)
        c_p2m(z, 1).start()

    @pl.loop(0, 4)
    def _(c):
        c_gd(c).wait_recv()
        for e in range(2):
            at = lanes(c * 2 + e, 256)
            gb_own[:, :, at] = gb_block(k, c * 2 + e) + gd_r[:, :, at].astype(F32)

    def c_y1p(h):
        return rc(y1p_s.at[h], y1p_r.at[h], I_Y1P + h, to_yp)

    def c_y1m(h):
        return rc(y1m_s.at[h], y1m_r.at[h], I_Y1M + h, to_ym)

    def c_y2p(h, e):
        return rc(y2p_s.at[h, e], y2p_r.at[h, e], I_Y2P + h * 2 + e, to_yp)

    def c_y2m(h, e):
        return rc(y2m_s.at[h, e], y2m_r.at[h, e], I_Y2M + h * 2 + e, to_ym)

    for h in (0, 1):
        s = y2 * 2 + zhs[h]
        y1p_s[h] = gb_own[s, 0:16, :].astype(BF)
        c_y1p(h).start()
        y1m_s[h] = gb_own[s, 16:32, :].astype(BF)
        c_y1m(h).start()
    for h in (0, 1):
        y2p_s[h, 1] = gb_own[yp * 2 + zhs[h], 16:32, :].astype(BF)
        c_y2p(h, 1).start()
        y2m_s[h, 0] = gb_own[ym * 2 + zhs[h], 0:16, :].astype(BF)
        c_y2m(h, 0).start()

    rc(darr.at[0:15], darr.at[0:15], I_DA, partner).wait_recv()
    total = darr[0]
    for i in range(1, 16):
        total = total + darr[i]
    dsum[...] = total
    dboth[k] = total
    c_db = rc(dsum, dboth.at[k], I_DB, partner)
    c_db.start()

    @pl.loop(0, 4)
    def _(z):
        for h in (0, 1):
            ga_own[z, h] = ga_block(h, z * 4 + x)

    for h in (0, 1):
        c_y1p(h).wait_recv()
        y2p_s[h, 0] = (
            gb_own[yp * 2 + zhs[h], 0:16, :] + y1p_r[h].astype(F32)
        ).astype(BF)
        c_y2p(h, 0).start()
        c_y1m(h).wait_recv()
        y2m_s[h, 1] = (
            gb_own[ym * 2 + zhs[h], 16:32, :] + y1m_r[h].astype(F32)
        ).astype(BF)
        c_y2m(h, 1).start()

    c_db.wait_recv()
    both = dboth[0] + dboth[1]
    ltile[...] = both
    lz[zh] = both
    c_dz = rc(ltile, lz.at[zh], I_DZ, dev(r, k, y * 2 + zhs[1]))
    c_dz.start()

    def c_oz(q):
        return rc(oz_s.at[q - 1], oz_r.at[q - 1], I_OZ + q - 1, dev(zq[q] * 4 + x, k, ft))

    def x_sum(z):
        for h in (0, 1):
            c_p2p(z, h).wait_recv()
            c_p2m(z, h).wait_recv()
        return ga_own[z] + p2p_r[z].astype(F32) + p2m_r[z].astype(F32)

    for q in (3, 2, 1):
        oz_s[q - 1] = x_sum(zq[q]).astype(BF)
        c_oz(q).start()

    def c_a2(t, h):
        to = lax.rem(r + t, 16)
        return rc(
            a2_s.at[h, to], gfin.at[h, r], I_A2 + h, dev(to, k, y * 2 + zhs[h])
        )

    for h in (1, 0):
        for e in (0, 1):
            c_y2p(h, e).wait_recv()
            c_y2m(h, e).wait_recv()

        @pl.loop(0, 16)
        def _(t):
            at = lanes(t, 128)
            s = y * 2 + zhs[h]
            for e in (0, 1):
                a2_s[h, t, e * 16:(e + 1) * 16, :] = (
                    gb_own[s, e * 16:(e + 1) * 16, at]
                    + y2p_r[h, e, :, at].astype(F32)
                    + y2m_r[h, e, :, at].astype(F32)
                ).astype(BF)

        if h == 0:
            gfin[0, r] = a2_s[0, r]

        @pl.loop(1 - h, 16)
        def _(t):
            c_a2(t, h).start()

    c_dz.wait_recv()
    lsum = lz[0] + lz[1]
    lzsum[...] = lsum
    ly[y] = lsum

    def c_dy(j):
        return rc(lzsum, ly.at[y], I_DY + j, dev(r, k, (yp, y2, ym)[j] * 2 + zh))

    for j in range(3):
        c_dy(j).start()

    own = x_sum(zl)
    for q in (1, 2, 3):
        c_oz(q).wait_recv()
        own = own + oz_r[q - 1].astype(F32)
    od_s[...] = own
    gfa[k] = od_s[k]
    c_od = rc(od_s.at[o], gfa.at[k], I_OD, partner)
    c_od.start()

    for j in range(3):
        c_dy(j).wait_recv()
    lall = ly[0] + ly[1] + ly[2] + ly[3]
    loss_out[0, 0] = jnp.sum(lall[5:6, :]) / F

    c_od.wait_recv()
    rc(gfin.at[0, 0:15], gfin.at[0, 0:15], I_A2, partner).wait_recv()
    rc(gfin.at[1], gfin.at[1], I_A2 + 1, partner).wait_recv()
    for half in range(2):
        at = slice(half * 256, (half + 1) * 256)
        st = dboth[half]
        ma_, inva_, mb_, invb_, c_ = (st[i:i + 1, :] for i in range(5))
        an = (a_in[:, at].astype(F32) - ma_) * inva_
        bn = (b_in[:, at].astype(F32) - mb_) * invb_
        d_ = -2.0 * (1.0 - c_)
        ga_out[:, at] = (inva_ * (d_ * (bn - c_ * an) + gfa[half])).astype(BF)
        gt = (
            gfin[0, half * 8:(half + 1) * 8].reshape(256, 128).astype(F32)
            + gfin[1, half * 8:(half + 1) * 8].reshape(256, 128).astype(F32)
        )
        gb_out[:, at] = (invb_ * (d_ * (an - c_ * bn) + gt.T)).astype(BF)

    c_v0.wait_send()
    rc(vbt.at[k, ft, :, 0:1920], vbt.at[k, ft, :, 0:1920], I_W1, partner).wait_send()
    w1_all[1].wait_send()
    for q in range(4):
        for c in (c_xp, c_xm, c_xpf, c_xmf):
            c(q).wait_send()
        if q:
            c_vz(q).wait_send()
            c_oz(q).wait_send()
    for h in (0, 1):
        for c in (c_yp, c_ym, c_ypf, c_ymf, c_y1p, c_y1m):
            c(h).wait_send()
        for j in range(4):
            c_wd(j, h).wait_send()
        for e in (0, 1):
            c_y2p(h, e).wait_send()
            c_y2m(h, e).wait_send()
    for z in range(4):
        c_p1p(z).wait_send()
        c_p1m(z).wait_send()
        c_gd(z).wait_send()
        for h in (0, 1):
            c_p2p(z, h).wait_send()
            c_p2m(z, h).wait_send()
    rc(darr.at[0:15], darr.at[0:15], I_DA, partner).wait_send()
    c_db.wait_send()
    c_dz.wait_send()
    for j in range(3):
        c_dy(j).wait_send()
    c_od.wait_send()
    rc(gfin.at[0, 0:15], gfin.at[0, 0:15], I_A2, partner).wait_send()
    rc(gfin.at[1], gfin.at[1], I_A2 + 1, partner).wait_send()


def shards(view_a, view_b):
    vm = pltpu.VMEM
    block = jax.ShapeDtypeStruct(view_a.shape, BF)
    ga, gb, loss = pl.pallas_call(
        kernel,
        out_shape=(block, block, jax.ShapeDtypeStruct((1, 1), F32)),
        in_specs=[pl.BlockSpec(memory_space=vm)] * 2,
        out_specs=(
            pl.BlockSpec(memory_space=vm),
            pl.BlockSpec(memory_space=vm),
            pl.BlockSpec(memory_space=pltpu.SMEM),
        ),
        scratch_shapes=[
            vm((2, 16, 128, 256), BF),
            vm((2, 8, 32, 2048), BF),
            vm((512, 128), BF),
            vm((8, 256), F32), vm((8, 256), F32),
            vm((256, 128), F32), vm((256, 128), F32),
            vm((256, 256), F32),
            vm((256, 256), BF), vm((256, 256), BF),
            vm((8, 256), F32), vm((256, 128), F32),
            vm((8, 256), F32), vm((16, 8, 256), F32),
            vm((8, 256), F32), vm((2, 8, 256), F32),
            vm((8, 256), F32), vm((2, 8, 256), F32),
            vm((8, 256), F32), vm((4, 8, 256), F32),
            vm((4, 128, 256), BF), vm((4, 128, 256), BF),
            vm((4, 128, 256), BF), vm((4, 128, 256), BF),
            vm((2, 4, 128, 256), F32),
            vm((4, 2, 128, 256), BF), vm((4, 2, 128, 256), BF),
            vm((4, 2, 128, 256), BF), vm((4, 2, 128, 256), BF),
            vm((4, 2, 128, 256), F32),
            vm((3, 2, 128, 256), BF), vm((3, 2, 128, 256), BF),
            vm((2, 128, 256), F32), vm((2, 128, 256), F32),
            vm((8, 32, 2048), BF), vm((8, 32, 2048), BF),
            vm((8, 32, 2048), F32),
            vm((2, 16, 2048), BF), vm((2, 16, 2048), BF),
            vm((2, 16, 2048), BF), vm((2, 16, 2048), BF),
            vm((2, 2, 16, 2048), BF), vm((2, 2, 16, 2048), BF),
            vm((2, 2, 16, 2048), BF), vm((2, 2, 16, 2048), BF),
            vm((2, 16, 32, 128), BF), vm((2, 16, 32, 128), BF),
            pltpu.SemaphoreType.DMA((N_SEM,)),
            pltpu.SemaphoreType.DMA((N_SEM,)),
        ],
        compiler_params=pltpu.CompilerParams(
            collective_id=0, has_side_effects=True, vmem_limit_bytes=56 * 1024 * 1024
        ),
    )(view_a, view_b)
    return ga, gb, loss.reshape(())


def solution(mesh):
    return jax.shard_map(
        shards,
        mesh=mesh,
        in_specs=(P("dp", "feat"), P("dp", "feat")),
        out_specs=(P("dp", "feat"), P("dp", "feat"), P()),
        check_vma=False,
    )
```

time: 413 us -> 85.7 us (0.21)
  waiting for transfers between devices: 268 us -> 0 us
  blocking collectives: 97.1 us -> 0 us
  Pallas kernels: 0 us -> 80.1 us
  between operations: 17 us -> 2.32 us
  matrix products: 9.24 us -> 0 us
  other arithmetic: 8.25 us -> 0 us
  starting transfers between devices: 7.48 us -> 0 us
    reduce_scatter x3 -> x0, waiting for transfers between devices: 199 us -> none  [the longest x1 89.4 us: shards(): grad_nb = lax.psum_scatter(partial_b, FEAT, scatter_dimension=1, tiled=True)]
    pallas_call x0 -> x1, Pallas kernels: none -> 80.1 us  [shards(): pl.pallas_call(kernel, out_shape=(block, block, jax.ShapeDtypeStruct((1,...]
    all_gather x1 -> x0, waiting for transfers between devices: 69.2 us -> none  [shards(): grad_full = lax.all_gather(grad_t, DP, axis=0, tiled=True)]
    all_to_all x2 -> x0, blocking collectives: 53.6 us -> none  [from_everyone(): return lax.all_to_all(copies, axis, split_axis=0, concat_axis=0, tiled=True)]
    psum x5 -> x0, blocking collectives: 43.5 us -> none  [over_axes(): x = lax.psum(x, axis)]
    dot_general x3 -> x0, matrix products: 9.24 us -> none  [the longest x1 5 us: shards(): lax.dot_general(a_half, grad_full, (((1,), (1,)), ((), ())), preferred_el...]
    all_to_all x1 -> x0, starting transfers between devices: 7.32 us -> none  [from_everyone(): return lax.all_to_all(copies, axis, split_axis=0, concat_axis=0, tiled=True)]
    reduce_sum x5 -> x0, other arithmetic: 4.86 us -> none  [the longest x1 2.43 us: shards(): jnp.sum((1.0 - unit) * corr_t * corr_t)]
  transfers between devices with their start and end apart: 5 -> 0, of which waited for: 4 -> 0; matrix products, arithmetic and copies ran while one was open for 1% -> 0% of each run, Pallas kernels for 0% -> 0%
where the time goes in v1:
time: 85.7 us; the launch traced here: 84.6 us
  Pallas kernels  80.1 us (93%)
  between operations  2.32 us (3%)
  local copies, waits for them, and re-layouts  2.26 us (3%)
    pallas_call x1, Pallas kernels, shards(): pl.pallas_call(kernel, out_shape=(block, block, jax.ShapeDtypeStruct((1,...  80.1 us
    unnamed x4, local copies, waits for them, and re-layouts  2.26 us

profile of v1, /device:TPU:1, one launch (start us, length us, event | category | flops | bytes accessed | tf_op | source)
XLA Modules:
  0.0 84.6 jit_solution(3239771705578817202)
XLA Ops:
  0.6 80.1 %shard_map.49 = (bf16[128,512]{1,0:T(8,128)(2,1)}, bf16[128,512]{1,0:T(8,128)(2,1)}, f32[1,1]{1,0:T(1,128)}) custom-call(bf16[128,512]{1,0:T(8,128)(2,1)} %a_in.1, bf16[128,512]{1,0:T(8,128)(2,1)} %b_in.1), custom_call_target="tpu_custom_call" | custom-call | tf_op jit(solution)/shard_map/pallas_call | solution.py:544
  80.7 0.0 copy-start
  80.7 1.6 %copy.8 = bf16[128,512]{1,0:T(8,128)(2,1)} copy(bf16[128,512]{1,0:T(8,128)(2,1)} %get-tuple-element.12) | data formatting | bytes 262144
  82.3 0.0 copy-done
  82.3 0.7 copy.9
Async XLA Ops:
  80.7 1.6 %copy-start = (bf16[128,512]{1,0:T(8,128)(2,1)S(1)}, bf16[128,512]{1,0:T(8,128)(2,1)}, u32[]{:S(2)}) copy-start(bf16[128,512]{1,0:T(8,128)(2,1)} %get-tuple-element.13) | copy-start | bytes 393220

commit v2 on v0

v2 whole, which is shorter than its diff:
```python
import jax
import jax.numpy as jnp
from jax import lax
from jax.experimental import pallas as pl
from jax.experimental.pallas import tpu as pltpu
from jax.sharding import PartitionSpec as P

F = 4096
S = 4096
EPS = 1e-05
LAMBDA = 0.0051
MESH = pl.DeviceIdType.MESH
BF = jnp.bfloat16
F32 = jnp.float32


class Slots:
    def __init__(self):
        self.used = 0

    def take(self, n):
        first = self.used
        self.used += n
        return first


SEM = Slots()
I_V1, I_W1 = (SEM.take(1) for _ in range(2))
I_GP, I_GM, I_GPF, I_GMF = (SEM.take(10) for _ in range(4))
I_ZP, I_ZM = (SEM.take(16) for _ in range(2))
I_WD = SEM.take(32)
I_SK, I_SX, I_SZ = SEM.take(1), SEM.take(3), SEM.take(3)
I_GD = SEM.take(4)
I_R1P, I_R1M = (SEM.take(10) for _ in range(2))
I_R2P, I_R2M = (SEM.take(20) for _ in range(2))
I_QP, I_QM = (SEM.take(16) for _ in range(2))
I_OZ, I_OX = (SEM.take(1) for _ in range(2))
I_LK, I_LX, I_LY, I_LZ = SEM.take(1), SEM.take(3), SEM.take(3), SEM.take(7)
N_SEM = SEM.used


def kernel(
    a_in, b_in, ga_out, gb_out, loss_out,
    at_loc, bt_loc, va, vb, stk, stx, stz, st1, st2, st3,
    asum, asq, bsum, bsq, raw, g1t, g2, cols,
    gaf, gd_s, gd_r, gbf, r1p_s, r1m_s, r1p_r, r1m_r, r2p_s, r2m_s, r2p_r, r2m_r,
    qp_s, qm_s, qp_r, qm_r, oz_s, fin_a, ox_s, fin_b,
    lt0, lt1, lt2, lt3, lk, lx, ly, lz, ssem, rsem,
):
    dp = lax.axis_index("dp")
    ft = lax.axis_index("feat")
    k = lax.rem(dp, 2)
    x = lax.rem(lax.div(dp, 2), 4)
    zl = lax.div(dp, 8)
    y, zh = lax.div(ft, 2), lax.rem(ft, 2)
    z = zh * 4 + zl
    o = 1 - k
    mb_slot = x * 4 + y
    xs = (x, lax.rem(x + 3, 4), lax.rem(x + 1, 4), lax.rem(x + 2, 4))
    ys = (y, lax.rem(y + 3, 4), lax.rem(y + 1, 4), lax.rem(y + 2, 4))
    _, xm, xp, x2 = xs
    _, ym, yp, y2 = ys

    def dev(x_, y_, z_, k_):
        return (lax.rem(z_, 4) * 8 + x_ * 2 + k_, y_ * 2 + lax.div(z_, 4))

    def zi(n):
        s = lax.rem(z + (n + 8), 8)
        return lax.div(s, 4), lax.rem(s, 4)

    def rc(src, dst, i, to):
        return pltpu.make_async_remote_copy(
            src_ref=src, dst_ref=dst, send_sem=ssem.at[i], recv_sem=rsem.at[i],
            device_id=to, device_id_type=MESH,
        )

    partner = dev(x, y, z, o)
    to_p = {"x": dev(xp, y, z, k), "y": dev(x, yp, z, k), "z": dev(x, y, lax.rem(z + 1, 8), k)}
    to_m = {"x": dev(xm, y, z, k), "y": dev(x, ym, z, k), "z": dev(x, y, lax.rem(z + 7, 8), k)}

    barrier = pltpu.get_barrier_semaphore()

    def greet(to):
        pl.semaphore_signal(barrier, inc=1, device_id=to, device_id_type=MESH)

    def plane(t):
        m = lax.rem(mb_slot + t, 16)
        return m, dev(lax.div(m, 4), lax.rem(m, 4), z, k)

    def pillar(t, k_):
        s = lax.rem(z + t, 8)
        return s, dev(x, y, s, k_)

    far_z = [(t, k_) for t in (4, 3, 5, 2, 6, 1, 7) for k_ in (k, o)] + [(0, o)]
    far_xy = (10, 14, 6, 9, 11, 2, 8, 5, 13, 7, 15, 3, 12, 4, 1)

    for t, k_ in far_z:
        greet(pillar(t, k_)[1])
    for t in far_xy:
        greet(plane(t)[1])

    for c in range(4):
        part = slice(c * 128, (c + 1) * 128)
        at_loc[2 * c:2 * c + 2] = a_in[:, part].astype(F32).T.astype(BF).reshape(2, 2, 32, 128)
    va[y, x, zh, zl, k] = at_loc[z, k]
    pl.semaphore_wait(barrier, 30)

    def c_v1(t, k_):
        s, to = pillar(t, k_)
        return rc(at_loc.at[s, k_], va.at[y, x, zh, zl, k], I_V1, to)

    def c_w1(t):
        m, to = plane(t)
        return rc(bt_loc.at[m], vb.at[zh, zl, k, y, x], I_W1, to)

    def all_pieces(i):
        return rc(bt_loc.at[0:15], bt_loc.at[0:15], i, partner)

    for t, k_ in far_z:
        c_v1(t, k_).start()
    for c in range(4):
        part = slice(c * 128, (c + 1) * 128)
        bt_loc[4 * c:4 * c + 4] = b_in[:, part].astype(F32).T.astype(BF).reshape(4, 32, 128)
    for t in far_xy:
        c_w1(t).start()
    vb[zh, zl, k, y, x] = bt_loc[mb_slot]

    af, bf = a_in[...].astype(F32), b_in[...].astype(F32)
    st1[...] = jnp.zeros_like(st1)
    for i, v in enumerate((af, af * af, bf, bf * bf, af * bf)):
        st1[i:i + 1, :] = jnp.sum(v, axis=0, keepdims=True)
    stk[k] = st1[...]
    c_sk = rc(st1, stk.at[k], I_SK, partner)
    c_sk.start()

    def ring_blocks(i):
        if i == 0:
            return "x", [va.at[y, xs[j], 0] for j in range(4)]
        if i < 5:
            return "x", [va.at[ys[i - 1], xs[j], 1] for j in range(4)]
        if i == 5:
            return "y", [va.at[ys[j], x, 1] for j in range(4)]
        return "y", [va.at[ys[j], xs[i - 6], 0] for j in range(4)]

    def c_gp(i):
        axis, b = ring_blocks(i)
        return rc(b[0], b[0], I_GP + i, to_p[axis])

    def c_gm(i):
        axis, b = ring_blocks(i)
        return rc(b[0], b[0], I_GM + i, to_m[axis])

    def c_gpf(i):
        axis, b = ring_blocks(i)
        return rc(b[1].at[0:2], b[1].at[0:2], I_GPF + i, to_p[axis])

    def c_gmf(i):
        axis, b = ring_blocks(i)
        return rc(b[2].at[2:4], b[2].at[2:4], I_GMF + i, to_m[axis])

    def ring_start(i):
        c_gp(i).start()
        c_gm(i).start()

    def ring_mid(i, then=None):
        c_gp(i).wait_recv()
        c_gpf(i).start()
        if then is not None:
            ring_start(then + 1)
        c_gm(i).wait_recv()
        c_gmf(i).start()
        if then is not None:
            ring_start(then + 2)

    def ring_end(i, then=None):
        c_gpf(i).wait_recv()
        c_gmf(i).wait_recv()
        if then is not None:
            ring_start(then + 3)

    def z_chunk(n, c):
        h_, l_ = zi(n)
        return vb.at[h_, l_, k, c]

    def c_zp(n, c):
        ref = z_chunk(-n, c)
        return rc(ref, ref, I_ZP + 4 * n + c, to_p["z"])

    def c_zm(n, c):
        ref = z_chunk(n, c)
        return rc(ref, ref, I_ZM + 4 * n + c, to_m["z"])

    def c_wd(n, c):
        ref = z_chunk(n, c)
        return rc(ref, ref, I_WD + (n % 8) * 4 + c, partner)

    def in_p(n, c):
        return n < 3 or (n == 3 and c < 2)

    def in_m(n, c):
        return n < 3 or (n == 3 and c >= 2)

    def z_step(n):
        for c in range(4):
            if in_p(n, c):
                c_zp(n, c).wait_recv()
                if in_p(n + 1, c):
                    c_zp(n + 1, c).start()
                c_wd(-(n + 1), c).start()
            if in_m(n, c):
                c_zm(n, c).wait_recv()
                if in_m(n + 1, c):
                    c_zm(n + 1, c).start()
                c_wd(n + 1, c).start()

    all_pieces(I_V1).wait_recv()
    ring_start(0)
    ring_start(5)
    ring_start(1)
    ring_start(6)
    all_pieces(I_W1).wait_recv()
    for c in range(4):
        c_zp(0, c).start()
        c_zm(0, c).start()
    for c in range(4):
        c_wd(0, c).start()

    c_sk.wait_recv()
    sk = stk[0] + stk[1]
    st2[...] = sk
    stx[x] = sk

    def c_sx(j):
        return rc(st2, stx.at[x], I_SX + j, dev((xm, xp, x2)[j], y, z, k))

    for j in range(3):
        c_sx(j).start()

    ring_mid(0, then=6)
    ring_mid(5, then=1)
    z_step(0)
    ring_end(0, then=6)
    ring_end(5, then=1)

    for j in range(3):
        c_sx(j).wait_recv()
    sx = (stx[0] + stx[1]) + (stx[2] + stx[3])
    st3[...] = sx
    stz[zl] = sx

    def c_sz(j):
        l_ = lax.rem(zl + (j + 1), 4)
        return rc(st3, stz.at[zl], I_SZ + j, dev(x, y, zh * 4 + l_, k))

    for j in range(3):
        c_sz(j).start()

    ring_mid(1)
    ring_mid(6)
    z_step(1)
    ring_mid(2)
    ring_mid(7)
    ring_mid(3)
    ring_mid(8)
    z_step(2)
    ring_mid(4)
    ring_mid(9)
    z_step(3)
    for i in (1, 6, 2, 7, 3, 8, 4, 9):
        ring_end(i)
    for n in range(8):
        for c in range(4):
            c_wd(n, c).wait_recv()

    for ref in (asum, asq, bsum, bsq, raw):
        ref[...] = jnp.zeros_like(ref)

    def va_at(x_, l_, kk):
        return va[:, x_, :, l_, kk].reshape(256, 128)

    def vb_at(x_, l_, kk):
        return vb[:, l_, kk, :, x_].reshape(256, 128)

    @pl.loop(0, 16)
    def _(t):
        x_, l_ = lax.div(t, 4), lax.rem(t, 4)
        a0, a1 = va_at(x_, l_, 0), va_at(x_, l_, 1)
        b0, b1 = vb_at(x_, l_, 0), vb_at(x_, l_, 1)
        raw[...] += lax.dot_general(
            jnp.concatenate([b0, b1], axis=1), jnp.concatenate([a0, a1], axis=1),
            (((1,), (1,)), ((), ())), preferred_element_type=F32,
        )
        for p0, p1, s_, q_ in ((a0, a1, asum, asq), (b0, b1, bsum, bsq)):
            f0, f1 = p0.astype(F32), p1.astype(F32)
            s_[...] += f0 + f1
            q_[...] += f0 * f0 + f1 * f1

    row = lax.broadcasted_iota(jnp.int32, (256, 256), 0)
    col = lax.broadcasted_iota(jnp.int32, (256, 256), 1)
    zero = jnp.zeros((256, 256), F32)
    eye = row == col

    def to_row(v):
        return jnp.sum(jnp.where(eye, v, zero), axis=0, keepdims=True)

    def to_col(v):
        return jnp.sum(jnp.where(eye, v, zero), axis=1, keepdims=True)

    ma = jnp.sum(asum[...], axis=1, keepdims=True) / S
    inva = lax.rsqrt(jnp.sum(asq[...], axis=1, keepdims=True) / S - ma * ma + EPS)
    mb = jnp.sum(bsum[...], axis=1, keepdims=True) / S
    invb = lax.rsqrt(jnp.sum(bsq[...], axis=1, keepdims=True) / S - mb * mb + EPS)
    ma_r, inva_r = to_row(ma), to_row(inva)
    ct = (raw[...] / S - mb * ma_r) * (invb * inva_r)

    def bits(v, shift, mask):
        return lax.bitwise_and(lax.shift_right_logical(v, shift), mask)

    j_id = (bits(row, 5, 3) * 2 + bits(row, 7, 1)) * 512 + mb_slot * 32 + bits(row, 0, 31)
    i_id = bits(col, 5, 7) * 512 + (z * 2 + k) * 32 + bits(col, 0, 31)
    unit = j_id == i_id
    g = jnp.where(unit, zero, (2.0 * LAMBDA) * ct)
    g1 = (invb * g).astype(BF).astype(F32)
    g1t[...] = g1.T.astype(BF)
    g2v = (g * inva_r).astype(BF)
    g2[...] = g2v
    gc = g * ct
    ua = inva * to_col(jnp.sum(gc, axis=0, keepdims=True))
    ub = invb * jnp.sum(gc, axis=1, keepdims=True)
    cols[:, 0:1] = ua
    cols[:, 1:2] = to_col(jnp.sum(g1 * mb, axis=0, keepdims=True)) - ma * ua
    cols[:, 2:3] = ub
    cols[:, 3:4] = jnp.sum(g2v.astype(F32) * ma_r, axis=1, keepdims=True) - mb * ub
    lv = jnp.sum(
        jnp.where(unit, (1.0 - ct) * (1.0 - ct), LAMBDA * ct * ct), axis=0, keepdims=True
    )
    l0 = jnp.broadcast_to(lv[:, 0:128] + lv[:, 128:256], (8, 128))
    lt0[...] = l0
    lk[k] = l0
    c_lk = rc(lt0, lk.at[k], I_LK, partner)
    c_lk.start()

    def near(j):
        return lax.rem(zl + (0, 1, 3, 2)[j], 4)

    def gb_pair(x_, l_, kk):
        a0, a1 = va_at(x_, l_, kk), va_at(x_ + 1, l_, kk)
        prod = jnp.dot(g2[...], jnp.concatenate([a0, a1], axis=1), preferred_element_type=F32)
        return [
            prod[:, e * 128:(e + 1) * 128]
            - vb_at(x_ + e, l_, kk).astype(F32) * cols[:, 2:3] - cols[:, 3:4]
            for e in (0, 1)
        ]

    def c_gd(j):
        return rc(gd_s.at[j], gd_r.at[j], I_GD + j, partner)

    for j in range(4):
        for x_ in (0, 2):
            for e, v in enumerate(gb_pair(x_, near(j), o)):
                gd_s[j, x_ + e] = v.astype(BF)
        c_gd(j).start()

    def ga_strip(x_):
        @pl.loop(0, 4)
        def _(l_):
            b01 = jnp.concatenate([vb_at(x_, l_, 0), vb_at(x_, l_, 1)], axis=1)
            prod = jnp.dot(g1t[...], b01, preferred_element_type=F32)
            for e in (0, 1):
                gaf[:, x_, :, l_, e] = (
                    prod[:, e * 128:(e + 1) * 128]
                    - va_at(x_, l_, e).astype(F32) * cols[:, 0:1] - cols[:, 1:2]
                ).reshape(4, 2, 32, 128)

    def axis_of(i):
        return "x" if i < 5 else "y"

    def part(i, j):
        if i == 0:
            return gaf[y, xs[j], 0]
        if i < 5:
            return gaf[ys[i - 1], xs[j], 1]
        if i == 5:
            return gaf[ys[j], x, 1]
        return gaf[ys[j], xs[i - 6], 0]

    def c_r1p(i):
        return rc(r1p_s.at[i], r1p_r.at[i], I_R1P + i, to_p[axis_of(i)])

    def c_r1m(i):
        return rc(r1m_s.at[i], r1m_r.at[i], I_R1M + i, to_m[axis_of(i)])

    def c_r2p(i, h):
        at = slice(2 * h, 2 * h + 2)
        return rc(r2p_s.at[i, at], r2p_r.at[i, at], I_R2P + 2 * i + h, to_p[axis_of(i)])

    def c_r2m(i, h):
        at = slice(2 * h, 2 * h + 2)
        return rc(r2m_s.at[i, at], r2m_r.at[i, at], I_R2M + 2 * i + h, to_m[axis_of(i)])

    def red_first(i):
        far = part(i, 3)
        r1p_s[i] = far[0:2].astype(BF)
        c_r1p(i).start()
        r1m_s[i] = far[2:4].astype(BF)
        c_r1m(i).start()

    def red_free(i):
        r2p_s[i, 2:4] = part(i, 2)[2:4].astype(BF)
        c_r2p(i, 1).start()
        r2m_s[i, 0:2] = part(i, 1)[0:2].astype(BF)
        c_r2m(i, 0).start()

    def red_mid(i):
        c_r1p(i).wait_recv()
        r2p_s[i, 0:2] = (part(i, 2)[0:2] + r1p_r[i].astype(F32)).astype(BF)
        c_r2p(i, 0).start()
        c_r1m(i).wait_recv()
        r2m_s[i, 2:4] = (part(i, 1)[2:4] + r1m_r[i].astype(F32)).astype(BF)
        c_r2m(i, 1).start()

    def red_end(i):
        for h in (0, 1):
            c_r2p(i, h).wait_recv()
            c_r2m(i, h).wait_recv()
        return part(i, 0) + r2p_r[i].astype(F32) + r2m_r[i].astype(F32)

    def gb_own(j):
        c_gd(j).wait_recv()
        for x_ in (0, 2):
            for e, v in enumerate(gb_pair(x_, near(j), k)):
                v = v + gd_r[j, x_ + e].astype(F32)
                gbf[:, near(j), :, x_ + e] = v.reshape(2, 4, 32, 128)

    def z_part(n, c):
        h_, l_ = zi(n)
        return gbf[h_, l_, c]

    def c_qp(n, c):
        return rc(qp_s.at[n, c], qp_r.at[n, c], I_QP + 4 * n + c, to_p["z"])

    def c_qm(n, c):
        return rc(qm_s.at[n, c], qm_r.at[n, c], I_QM + 4 * n + c, to_m["z"])

    def q_send(n, first):
        for c in range(4):
            if in_p(3 - n, c) and in_p(4 - n, c) != first:
                v = z_part(4 - n, c)
                if not first:
                    c_qp(n - 1, c).wait_recv()
                    v = v + qp_r[n - 1, c].astype(F32)
                qp_s[n, c] = v.astype(BF)
                c_qp(n, c).start()
            if in_m(3 - n, c) and in_m(4 - n, c) != first:
                v = z_part(n - 4, c)
                if not first:
                    c_qm(n - 1, c).wait_recv()
                    v = v + qm_r[n - 1, c].astype(F32)
                qm_s[n, c] = v.astype(BF)
                c_qm(n, c).start()

    ga_strip(x2)
    red_first(9)
    for i in (4, 3, 2, 1):
        red_first(i)
    gb_own(0)
    q_send(0, True)
    gb_own(1)
    gb_own(2)
    q_send(1, True)
    gb_own(3)
    ga_strip(xp)
    red_first(8)
    ga_strip(xm)
    red_first(7)
    for i in (9, 4, 8, 7, 3, 2, 1):
        red_free(i)
    ga_strip(x)
    red_first(6)
    red_free(6)
    red_mid(9)
    red_mid(4)
    q_send(1, False)
    red_mid(8)
    red_mid(3)
    red_mid(7)
    red_mid(2)

    def c_lx(j):
        return rc(lt1, lx.at[x], I_LX + j, dev((xm, xp, x2)[j], y, z, k))

    def c_ly(j):
        return rc(lt2, ly.at[y], I_LY + j, dev(x, (ym, yp, y2)[j], z, k))

    def c_lz(j):
        return rc(lt3, lz.at[z], I_LZ + j, pillar(j + 1, k)[1])

    c_lk.wait_recv()
    l1 = lk[0] + lk[1]
    lt1[...] = l1
    lx[x] = l1
    for j in range(3):
        c_lx(j).start()

    gaf[y, x2, 0] = red_end(9)
    red_first(0)
    gaf[y2, x, 1] = red_end(4)
    red_first(5)
    red_mid(6)
    red_mid(1)
    q_send(2, False)
    gaf[y, xp, 0] = red_end(8)
    gaf[y, xm, 0] = red_end(7)
    red_free(0)
    gaf[yp, x, 1] = red_end(3)
    gaf[ym, x, 1] = red_end(2)
    red_free(5)
    red_mid(0)
    red_mid(5)
    for j in range(3):
        c_lx(j).wait_recv()
    l2 = (lx[0] + lx[1]) + (lx[2] + lx[3])
    lt2[...] = l2
    ly[y] = l2
    for j in range(3):
        c_ly(j).start()
    q_send(3, False)
    gaf[y, x, 0] = red_end(6)
    gaf[y, x, 1] = red_end(1)

    def c_ox(t):
        m, to = plane(t)
        return rc(ox_s.at[m], fin_b.at[mb_slot], I_OX, to)

    for c in range(4):
        c_qp(3, c).wait_recv()
        c_qm(3, c).wait_recv()
        v = z_part(0, c) + qp_r[3, c].astype(F32) + qm_r[3, c].astype(F32)
        for x_ in range(4):
            ox_s[x_ * 4 + c] = v[x_].astype(BF)
    for t in far_xy:
        c_ox(t).start()
    fin_b[mb_slot] = ox_s[mb_slot]
    for j in range(3):
        c_ly(j).wait_recv()
    l3 = (ly[0] + ly[1]) + (ly[2] + ly[3])
    lt3[...] = l3
    lz[z] = l3
    for j in range(7):
        c_lz(j).start()

    def c_oz(t, k_):
        s, to = pillar(t, k_)
        return rc(oz_s.at[s, k_], fin_a.at[z, k], I_OZ, to)

    oz_s[0:4] = red_end(0).astype(BF)
    oz_s[4:8] = red_end(5).astype(BF)
    for t, k_ in far_z:
        c_oz(t, k_).start()
    fin_a[z, k] = oz_s[z, k]

    for j in range(3):
        c_sz(j).wait_recv()
    st = ((stz[0] + stz[1]) + (stz[2] + stz[3])) / S
    ma_, mb_ = st[0:1], st[2:3]
    inva_ = lax.rsqrt(st[1:2] - ma_ * ma_ + EPS)
    invb_ = lax.rsqrt(st[3:4] - mb_ * mb_ + EPS)
    c_ = (st[4:5] - ma_ * mb_) * (inva_ * invb_)
    d_ = -2.0 * (1.0 - c_)

    for j in range(7):
        c_lz(j).wait_recv()
    lall = lz[0]
    for i in range(1, 8):
        lall = lall + lz[i]
    loss_out[0, 0] = jnp.sum(lall[0:1, :]) / F

    all_pieces(I_OX).wait_recv()
    for c in range(4):
        at = slice(c * 128, (c + 1) * 128)
        an = (a_in[:, at].astype(F32) - ma_[:, at]) * inva_[:, at]
        bn = (b_in[:, at].astype(F32) - mb_[:, at]) * invb_[:, at]
        gt = fin_b[4 * c:4 * c + 4].reshape(128, 128).astype(F32).T
        gb_out[:, at] = (invb_[:, at] * (d_[:, at] * (an - c_[:, at] * bn) + gt)).astype(BF)

    all_pieces(I_OZ).wait_recv()
    for c in range(4):
        at = slice(c * 128, (c + 1) * 128)
        an = (a_in[:, at].astype(F32) - ma_[:, at]) * inva_[:, at]
        bn = (b_in[:, at].astype(F32) - mb_[:, at]) * invb_[:, at]
        gt = fin_a[2 * c:2 * c + 2].reshape(128, 128).astype(F32).T
        ga_out[:, at] = (inva_[:, at] * (d_[:, at] * (bn - c_[:, at] * an) + gt)).astype(BF)

    for c in (c_sk, c_lk):
        c.wait_send()
    for i in (I_V1, I_W1, I_OX, I_OZ):
        all_pieces(i).wait_send()
    for j in range(3):
        for c in (c_sx, c_sz, c_lx, c_ly):
            c(j).wait_send()
    for j in range(7):
        c_lz(j).wait_send()
    for i in range(4):
        c_gd(i).wait_send()
    for i in range(10):
        for c in (c_gp, c_gm, c_gpf, c_gmf, c_r1p, c_r1m):
            c(i).wait_send()
        for h in (0, 1):
            c_r2p(i, h).wait_send()
            c_r2m(i, h).wait_send()
    for n in range(8):
        for c in range(4):
            c_wd(n, c).wait_send()
    for n in range(4):
        for c in range(4):
            if in_p(n, c):
                c_zp(n, c).wait_send()
            if in_m(n, c):
                c_zm(n, c).wait_send()
            if in_p(3 - n, c):
                c_qp(n, c).wait_send()
            if in_m(3 - n, c):
                c_qm(n, c).wait_send()


def shards(view_a, view_b):
    vm = pltpu.VMEM
    block = jax.ShapeDtypeStruct(view_a.shape, BF)
    ga, gb, loss = pl.pallas_call(
        kernel,
        out_shape=(block, block, jax.ShapeDtypeStruct((1, 1), F32)),
        in_specs=[pl.BlockSpec(memory_space=vm)] * 2,
        out_specs=(
            pl.BlockSpec(memory_space=vm),
            pl.BlockSpec(memory_space=vm),
            pl.BlockSpec(memory_space=pltpu.SMEM),
        ),
        scratch_shapes=[
            vm((8, 2, 32, 128), BF), vm((16, 32, 128), BF),
            vm((4, 4, 2, 4, 2, 32, 128), BF),
            vm((2, 4, 2, 4, 4, 32, 128), BF),
            vm((2, 8, 512), F32), vm((4, 8, 512), F32), vm((4, 8, 512), F32),
            vm((8, 512), F32), vm((8, 512), F32), vm((8, 512), F32),
            *[vm((256, 128), F32)] * 4,
            vm((256, 256), F32), vm((256, 256), BF), vm((256, 256), BF),
            vm((256, 128), F32),
            vm((4, 4, 2, 4, 2, 32, 128), F32),
            vm((4, 4, 256, 128), BF), vm((4, 4, 256, 128), BF),
            vm((2, 4, 4, 4, 32, 128), F32),
            *[vm((10, 2, 2, 32, 128), BF)] * 4,
            *[vm((10, 4, 2, 32, 128), BF)] * 4,
            *[vm((4, 4, 4, 32, 128), BF)] * 4,
            vm((8, 2, 32, 128), BF), vm((8, 2, 32, 128), BF),
            vm((16, 32, 128), BF), vm((16, 32, 128), BF),
            *[vm((8, 128), F32)] * 4,
            vm((2, 8, 128), F32), vm((4, 8, 128), F32), vm((4, 8, 128), F32), vm((8, 8, 128), F32),
            pltpu.SemaphoreType.DMA((N_SEM,)),
            pltpu.SemaphoreType.DMA((N_SEM,)),
        ],
        compiler_params=pltpu.CompilerParams(
            collective_id=0, has_side_effects=True, vmem_limit_bytes=56 * 1024 * 1024
        ),
    )(view_a, view_b)
    return ga, gb, loss.reshape(())


def solution(mesh):
    return jax.shard_map(
        shards,
        mesh=mesh,
        in_specs=(P("dp", "feat"), P("dp", "feat")),
        out_specs=(P("dp", "feat"), P("dp", "feat"), P()),
        check_vma=False,
    )
```

time: 413 us -> 77.3 us (0.19)
  waiting for transfers between devices: 268 us -> 0 us
  blocking collectives: 97.1 us -> 0 us
  Pallas kernels: 0 us -> 72.6 us
  between operations: 17 us -> 2.32 us
  matrix products: 9.24 us -> 0 us
  other arithmetic: 8.25 us -> 0 us
  starting transfers between devices: 7.48 us -> 0 us
    reduce_scatter x3 -> x0, waiting for transfers between devices: 199 us -> none  [the longest x1 89.4 us: shards(): grad_nb = lax.psum_scatter(partial_b, FEAT, scatter_dimension=1, tiled=True)]
    pallas_call x0 -> x1, Pallas kernels: none -> 72.6 us  [shards(): pl.pallas_call(kernel, out_shape=(block, block, jax.ShapeDtypeStruct((1,...]
    all_gather x1 -> x0, waiting for transfers between devices: 69.2 us -> none  [shards(): grad_full = lax.all_gather(grad_t, DP, axis=0, tiled=True)]
    all_to_all x2 -> x0, blocking collectives: 53.6 us -> none  [from_everyone(): return lax.all_to_all(copies, axis, split_axis=0, concat_axis=0, tiled=True)]
    psum x5 -> x0, blocking collectives: 43.5 us -> none  [over_axes(): x = lax.psum(x, axis)]
    dot_general x3 -> x0, matrix products: 9.24 us -> none  [the longest x1 5 us: shards(): lax.dot_general(a_half, grad_full, (((1,), (1,)), ((), ())), preferred_el...]
    all_to_all x1 -> x0, starting transfers between devices: 7.32 us -> none  [from_everyone(): return lax.all_to_all(copies, axis, split_axis=0, concat_axis=0, tiled=True)]
    reduce_sum x5 -> x0, other arithmetic: 4.86 us -> none  [the longest x1 2.43 us: shards(): jnp.sum((1.0 - unit) * corr_t * corr_t)]
  transfers between devices with their start and end apart: 5 -> 0, of which waited for: 4 -> 0; matrix products, arithmetic and copies ran while one was open for 1% -> 0% of each run, Pallas kernels for 0% -> 0%
where the time goes in v2:
time: 77.3 us; the launch traced here: 77.2 us
  Pallas kernels  72.6 us (94%)
  between operations  2.32 us (3%)
  local copies, waits for them, and re-layouts  2.26 us (3%)
    pallas_call x1, Pallas kernels, shards(): pl.pallas_call(kernel, out_shape=(block, block, jax.ShapeDtypeStruct((1,...  72.6 us
    unnamed x4, local copies, waits for them, and re-layouts  2.26 us

profile of v2, /device:TPU:1, one launch (start us, length us, event | category | flops | bytes accessed | tf_op | source)
XLA Modules:
  0.0 77.2 jit_solution(17532852535357553398)
XLA Ops:
  0.6 72.6 %shard_map.49 = (bf16[128,512]{1,0:T(8,128)(2,1)}, bf16[128,512]{1,0:T(8,128)(2,1)}, f32[1,1]{1,0:T(1,128)}) custom-call(bf16[128,512]{1,0:T(8,128)(2,1)} %a_in.1, bf16[128,512]{1,0:T(8,128)(2,1)} %b_in.1), custom_call_target="tpu_custom_call" | custom-call | tf_op jit(solution)/shard_map/pallas_call | solution.py:629
  73.2 0.0 copy-start
  73.3 1.6 %copy.8 = bf16[128,512]{1,0:T(8,128)(2,1)} copy(bf16[128,512]{1,0:T(8,128)(2,1)} %get-tuple-element.12) | data formatting | bytes 262144
  74.9 0.0 copy-done
  74.9 0.7 copy.9
Async XLA Ops:
  73.2 1.6 %copy-start = (bf16[128,512]{1,0:T(8,128)(2,1)S(1)}, bf16[128,512]{1,0:T(8,128)(2,1)}, u32[]{:S(2)}) copy-start(bf16[128,512]{1,0:T(8,128)(2,1)} %get-tuple-element.13) | copy-start | bytes 393220

commit v3 on v2

--- a/solution.py
+++ b/solution.py
@@ -25,27 +25,28 @@
 
 
 SEM = Slots()
-I_V1, I_W1 = (SEM.take(1) for _ in range(2))
-I_GP, I_GM, I_GPF, I_GMF = (SEM.take(10) for _ in range(4))
-I_ZP, I_ZM = (SEM.take(16) for _ in range(2))
-I_WD = SEM.take(32)
-I_SK, I_SX, I_SZ = SEM.take(1), SEM.take(3), SEM.take(3)
+I_V1, I_W1, I_SK, I_SX, I_SZ, I_OZ, I_OX, I_LK, I_LX, I_LY, I_LZ = (SEM.take(1) for _ in range(11))
+I_GP, I_GM, I_GF = (SEM.take(10) for _ in range(3))
+I_ZP, I_ZM = (SEM.take(14) for _ in range(2))
+I_WD = SEM.take(8)
 I_GD = SEM.take(4)
-I_R1P, I_R1M = (SEM.take(10) for _ in range(2))
-I_R2P, I_R2M = (SEM.take(20) for _ in range(2))
-I_QP, I_QM = (SEM.take(16) for _ in range(2))
-I_OZ, I_OX = (SEM.take(1) for _ in range(2))
-I_LK, I_LX, I_LY, I_LZ = SEM.take(1), SEM.take(3), SEM.take(3), SEM.take(7)
-N_SEM = SEM.used
+I_R1P, I_R1M, I_R2 = (SEM.take(10) for _ in range(3))
+I_QP, I_QM = (SEM.take(14) for _ in range(2))
+N_RECV = SEM.used
+OUT = Slots()
+(O_V1, O_W1, O_SK, O_SX, O_SZ, O_OZ, O_OX, O_LK, O_LX, O_LY, O_LZ,
+ O_GP, O_GM, O_GPF, O_GMF, O_WD, O_GD, O_R1P, O_R1M, O_R2P, O_R2M) = (OUT.take(1) for _ in range(21))
+O_ZP, O_ZM, O_QP, O_QM = (OUT.take(2) for _ in range(4))
+N_SEND = OUT.used
 
 
 def kernel(
-    a_in, b_in, ga_out, gb_out, loss_out,
-    at_loc, bt_loc, va, vb, stk, stx, stz, st1, st2, st3,
+    a_hbm, b_hbm, ga_out, gb_out, loss_out,
+    a_in, b_in, at_loc, bt_loc, va, vb, stk, stx, stz, st1, st2, st3,
     asum, asq, bsum, bsq, raw, g1t, g2, cols,
     gaf, gd_s, gd_r, gbf, r1p_s, r1m_s, r1p_r, r1m_r, r2p_s, r2m_s, r2p_r, r2m_r,
     qp_s, qm_s, qp_r, qm_r, oz_s, fin_a, ox_s, fin_b,
-    lt0, lt1, lt2, lt3, lk, lx, ly, lz, ssem, rsem,
+    lt0, lt1, lt2, lt3, lk, lx, ly, lz, ssem, rsem, isem,
 ):
     dp = lax.axis_index("dp")
     ft = lax.axis_index("feat")
@@ -68,11 +69,17 @@
         s = lax.rem(z + (n + 8), 8)
         return lax.div(s, 4), lax.rem(s, 4)
 
-    def rc(src, dst, i, to):
+    def rc(src, dst, i, e, to):
         return pltpu.make_async_remote_copy(
-            src_ref=src, dst_ref=dst, send_sem=ssem.at[i], recv_sem=rsem.at[i],
+            src_ref=src, dst_ref=dst, send_sem=ssem.at[e], recv_sem=rsem.at[i],
             device_id=to, device_id_type=MESH,
         )
+
+    def landed(ref, i):
+        rc(ref, ref, i, 0, partner).wait_recv()
+
+    def left(ref, e):
+        rc(ref, ref, 0, e, partner).wait_send()
 
     partner = dev(x, y, z, o)
     to_p = {"x": dev(xp, y, z, k), "y": dev(x, yp, z, k), "z": dev(x, y, lax.rem(z + 1, 8), k)}
@@ -90,6 +97,11 @@
     def pillar(t, k_):
         s = lax.rem(z + t, 8)
         return s, dev(x, y, s, k_)
+
+    load_a = pltpu.make_async_copy(a_hbm, a_in, isem.at[0])
+    load_b = pltpu.make_async_copy(b_hbm, b_in, isem.at[1])
+    load_a.start()
+    load_b.start()
 
     far_z = [(t, k_) for t in (4, 3, 5, 2, 6, 1, 7) for k_ in (k, o)] + [(0, o)]
     far_xy = (10, 14, 6, 9, 11, 2, 8, 5, 13, 7, 15, 3, 12, 4, 1)
@@ -99,6 +111,7 @@
     for t in far_xy:
         greet(plane(t)[1])
 
+    load_a.wait()
     for c in range(4):
         part = slice(c * 128, (c + 1) * 128)
         at_loc[2 * c:2 * c + 2] = a_in[:, part].astype(F32).T.astype(BF).reshape(2, 2, 32, 128)
@@ -107,17 +120,15 @@
 
     def c_v1(t, k_):
         s, to = pillar(t, k_)
-        return rc(at_loc.at[s, k_], va.at[y, x, zh, zl, k], I_V1, to)
+        return rc(at_loc.at[s, k_], va.at[y, x, zh, zl, k], I_V1, O_V1, to)
 
     def c_w1(t):
         m, to = plane(t)
-        return rc(bt_loc.at[m], vb.at[zh, zl, k, y, x], I_W1, to)
-
-    def all_pieces(i):
-        return rc(bt_loc.at[0:15], bt_loc.at[0:15], i, partner)
+        return rc(bt_loc.at[m], vb.at[zh, zl, k, y, x], I_W1, O_W1, to)
 
     for t, k_ in far_z:
         c_v1(t, k_).start()
+    load_b.wait()
     for c in range(4):
         part = slice(c * 128, (c + 1) * 128)
         bt_loc[4 * c:4 * c + 4] = b_in[:, part].astype(F32).T.astype(BF).reshape(4, 32, 128)
@@ -130,7 +141,7 @@
     for i, v in enumerate((af, af * af, bf, bf * bf, af * bf)):
         st1[i:i + 1, :] = jnp.sum(v, axis=0, keepdims=True)
     stk[k] = st1[...]
-    c_sk = rc(st1, stk.at[k], I_SK, partner)
+    c_sk = rc(st1, stk.at[k], I_SK, O_SK, partner)
     c_sk.start()
 
     def ring_blocks(i):
@@ -144,19 +155,19 @@
 
     def c_gp(i):
         axis, b = ring_blocks(i)
-        return rc(b[0], b[0], I_GP + i, to_p[axis])
+        return rc(b[0], b[0], I_GP + i, O_GP, to_p[axis])
 
     def c_gm(i):
         axis, b = ring_blocks(i)
-        return rc(b[0], b[0], I_GM + i, to_m[axis])
+        return rc(b[0], b[0], I_GM + i, O_GM, to_m[axis])
 
     def c_gpf(i):
         axis, b = ring_blocks(i)
-        return rc(b[1].at[0:2], b[1].at[0:2], I_GPF + i, to_p[axis])
+        return rc(b[1].at[0:2], b[1].at[0:2], I_GF + i, O_GPF, to_p[axis])
 
     def c_gmf(i):
         axis, b = ring_blocks(i)
-        return rc(b[2].at[2:4], b[2].at[2:4], I_GMF + i, to_m[axis])
+        return rc(b[2].at[2:4], b[2].at[2:4], I_GF + i, O_GMF, to_m[axis])
 
     def ring_start(i):
         c_gp(i).start()
@@ -173,8 +184,7 @@
             ring_start(then + 2)
 
     def ring_end(i, then=None):
-        c_gpf(i).wait_recv()
-        c_gmf(i).wait_recv()
+        landed(ring_blocks(i)[1][3], I_GF + i)
         if then is not None:
             ring_start(then + 3)
 
@@ -184,15 +194,15 @@
 
     def c_zp(n, c):
         ref = z_chunk(-n, c)
-        return rc(ref, ref, I_ZP + 4 * n + c, to_p["z"])
+        return rc(ref, ref, I_ZP + 4 * n + c, O_ZP + n // 3, to_p["z"])
 
     def c_zm(n, c):
         ref = z_chunk(n, c)
-        return rc(ref, ref, I_ZM + 4 * n + c, to_m["z"])
+        return rc(ref, ref, I_ZM + 4 * n + c - 2 * (n // 3), O_ZM + n // 3, to_m["z"])
 
     def c_wd(n, c):
         ref = z_chunk(n, c)
-        return rc(ref, ref, I_WD + (n % 8) * 4 + c, partner)
+        return rc(ref, ref, I_WD + n % 8, O_WD, partner)
 
     def in_p(n, c):
         return n < 3 or (n == 3 and c < 2)
@@ -213,12 +223,12 @@
                     c_zm(n + 1, c).start()
                 c_wd(n + 1, c).start()
 
-    all_pieces(I_V1).wait_recv()
+    landed(bt_loc.at[0:15], I_V1)
     ring_start(0)
     ring_start(5)
     ring_start(1)
     ring_start(6)
-    all_pieces(I_W1).wait_recv()
+    landed(bt_loc.at[0:15], I_W1)
     for c in range(4):
         c_zp(0, c).start()
         c_zm(0, c).start()
@@ -231,7 +241,7 @@
     stx[x] = sk
 
     def c_sx(j):
-        return rc(st2, stx.at[x], I_SX + j, dev((xm, xp, x2)[j], y, z, k))
+        return rc(st2, stx.at[x], I_SX, O_SX, dev((xm, xp, x2)[j], y, z, k))
 
     for j in range(3):
         c_sx(j).start()
@@ -242,18 +252,49 @@
     ring_end(0, then=6)
     ring_end(5, then=1)
 
-    for j in range(3):
-        c_sx(j).wait_recv()
+    landed(stx.at[0:3], I_SX)
     sx = (stx[0] + stx[1]) + (stx[2] + stx[3])
     st3[...] = sx
     stz[zl] = sx
 
     def c_sz(j):
         l_ = lax.rem(zl + (j + 1), 4)
-        return rc(st3, stz.at[zl], I_SZ + j, dev(x, y, zh * 4 + l_, k))
+        return rc(st3, stz.at[zl], I_SZ, O_SZ, dev(x, y, zh * 4 + l_, k))
 
     for j in range(3):
         c_sz(j).start()
+
+    for ref in (asum, asq, bsum, bsq, raw):
+        ref[...] = jnp.zeros_like(ref)
+
+    def va_at(x_, l_, kk):
+        return va[:, x_, :, l_, kk].reshape(256, 128)
+
+    def vb_at(x_, l_, kk):
+        return vb[:, l_, kk, :, x_].reshape(256, 128)
+
+    def near(j):
+        return lax.rem(zl + (0, 1, 3, 2)[j], 4)
+
+    def corr(j):
+        l_ = near(j)
+
+        pairs = [(x_, kk) for x_ in range(4) for kk in (0, 1)]
+        a_, b_ = ([f(x_, l_, kk) for x_, kk in pairs] for f in (va_at, vb_at))
+        raw[...] += lax.dot_general(
+            jnp.concatenate(b_, axis=1), jnp.concatenate(a_, axis=1),
+            (((1,), (1,)), ((), ())), preferred_element_type=F32,
+        )
+        for f, s_, q_ in ((va_at, asum, asq), (vb_at, bsum, bsq)):
+            for h in range(4):
+                at = slice(h * 64, h * 64 + 64)
+                v = [f(x_, l_, kk)[at].astype(F32) for x_, kk in pairs]
+                s_[at, :] += sum(v[1:], v[0])
+                q_[at, :] += sum((u * u for u in v[1:]), v[0] * v[0])
+
+    def from_core(n):
+        h_, l_ = zi(n)
+        landed(vb.at[h_, l_, o], I_WD + n % 8)
 
     ring_mid(1)
     ring_mid(6)
@@ -265,36 +306,21 @@
     z_step(2)
     ring_mid(4)
     ring_mid(9)
-    z_step(3)
     for i in (1, 6, 2, 7, 3, 8, 4, 9):
         ring_end(i)
-    for n in range(8):
-        for c in range(4):
-            c_wd(n, c).wait_recv()
-
-    for ref in (asum, asq, bsum, bsq, raw):
-        ref[...] = jnp.zeros_like(ref)
-
-    def va_at(x_, l_, kk):
-        return va[:, x_, :, l_, kk].reshape(256, 128)
-
-    def vb_at(x_, l_, kk):
-        return vb[:, l_, kk, :, x_].reshape(256, 128)
-
-    @pl.loop(0, 16)
-    def _(t):
-        x_, l_ = lax.div(t, 4), lax.rem(t, 4)
-        a0, a1 = va_at(x_, l_, 0), va_at(x_, l_, 1)
-        b0, b1 = vb_at(x_, l_, 0), vb_at(x_, l_, 1)
-        raw[...] += lax.dot_general(
-            jnp.concatenate([b0, b1], axis=1), jnp.concatenate([a0, a1], axis=1),
-            (((1,), (1,)), ((), ())), preferred_element_type=F32,
-        )
-        for p0, p1, s_, q_ in ((a0, a1, asum, asq), (b0, b1, bsum, bsq)):
-            f0, f1 = p0.astype(F32), p1.astype(F32)
-            s_[...] += f0 + f1
-            q_[...] += f0 * f0 + f1 * f1
-
+    z_step(3)
+    from_core(2)
+    from_core(-2)
+    corr(3)
+    from_core(1)
+    from_core(-3)
+    corr(1)
+    from_core(-1)
+    from_core(3)
+    corr(2)
+    from_core(0)
+    from_core(4)
+    corr(0)
     row = lax.broadcasted_iota(jnp.int32, (256, 256), 0)
     col = lax.broadcasted_iota(jnp.int32, (256, 256), 1)
     zero = jnp.zeros((256, 256), F32)
@@ -337,11 +363,8 @@
     l0 = jnp.broadcast_to(lv[:, 0:128] + lv[:, 128:256], (8, 128))
     lt0[...] = l0
     lk[k] = l0
-    c_lk = rc(lt0, lk.at[k], I_LK, partner)
+    c_lk = rc(lt0, lk.at[k], I_LK, O_LK, partner)
     c_lk.start()
-
-    def near(j):
-        return lax.rem(zl + (0, 1, 3, 2)[j], 4)
 
     def gb_pair(x_, l_, kk):
         a0, a1 = va_at(x_, l_, kk), va_at(x_ + 1, l_, kk)
@@ -353,7 +376,7 @@
         ]
 
     def c_gd(j):
-        return rc(gd_s.at[j], gd_r.at[j], I_GD + j, partner)
+        return rc(gd_s.at[j], gd_r.at[j], I_GD + j, O_GD, partner)
 
     for j in range(4):
         for x_ in (0, 2):
@@ -385,18 +408,18 @@
         return gaf[ys[j], xs[i - 6], 0]
 
     def c_r1p(i):
-        return rc(r1p_s.at[i], r1p_r.at[i], I_R1P + i, to_p[axis_of(i)])
+        return rc(r1p_s.at[i], r1p_r.at[i], I_R1P + i, O_R1P, to_p[axis_of(i)])
 
     def c_r1m(i):
-        return rc(r1m_s.at[i], r1m_r.at[i], I_R1M + i, to_m[axis_of(i)])
+        return rc(r1m_s.at[i], r1m_r.at[i], I_R1M + i, O_R1M, to_m[axis_of(i)])
 
     def c_r2p(i, h):
         at = slice(2 * h, 2 * h + 2)
-        return rc(r2p_s.at[i, at], r2p_r.at[i, at], I_R2P + 2 * i + h, to_p[axis_of(i)])
+        return rc(r2p_s.at[i, at], r2p_r.at[i, at], I_R2 + i, O_R2P, to_p[axis_of(i)])
 
     def c_r2m(i, h):
         at = slice(2 * h, 2 * h + 2)
-        return rc(r2m_s.at[i, at], r2m_r.at[i, at], I_R2M + 2 * i + h, to_m[axis_of(i)])
+        return rc(r2m_s.at[i, at], r2m_r.at[i, at], I_R2 + i, O_R2M, to_m[axis_of(i)])
 
     def red_first(i):
         far = part(i, 3)
@@ -420,9 +443,7 @@
         c_r2m(i, 1).start()
 
     def red_end(i):
-        for h in (0, 1):
-            c_r2p(i, h).wait_recv()
-            c_r2m(i, h).wait_recv()
+        landed(r2p_r.at[0:2], I_R2 + i)
         return part(i, 0) + r2p_r[i].astype(F32) + r2m_r[i].astype(F32)
 
     def gb_own(j):
@@ -437,10 +458,10 @@
         return gbf[h_, l_, c]
 
     def c_qp(n, c):
-        return rc(qp_s.at[n, c], qp_r.at[n, c], I_QP + 4 * n + c, to_p["z"])
+        return rc(qp_s.at[n, c], qp_r.at[n, c], I_QP + 4 * n + c - 2 * min(n, 1), O_QP + min(n, 1), to_p["z"])
 
     def c_qm(n, c):
-        return rc(qm_s.at[n, c], qm_r.at[n, c], I_QM + 4 * n + c, to_m["z"])
+        return rc(qm_s.at[n, c], qm_r.at[n, c], I_QM + 4 * n + c - 2, O_QM + min(n, 1), to_m["z"])
 
     def q_send(n, first):
         for c in range(4):
@@ -487,13 +508,13 @@
     red_mid(2)
 
     def c_lx(j):
-        return rc(lt1, lx.at[x], I_LX + j, dev((xm, xp, x2)[j], y, z, k))
+        return rc(lt1, lx.at[x], I_LX, O_LX, dev((xm, xp, x2)[j], y, z, k))
 
     def c_ly(j):
-        return rc(lt2, ly.at[y], I_LY + j, dev(x, (ym, yp, y2)[j], z, k))
+        return rc(lt2, ly.at[y], I_LY, O_LY, dev(x, (ym, yp, y2)[j], z, k))
 
     def c_lz(j):
-        return rc(lt3, lz.at[z], I_LZ + j, pillar(j + 1, k)[1])
+        return rc(lt3, lz.at[z], I_LZ, O_LZ, pillar(j + 1, k)[1])
 
     c_lk.wait_recv()
     l1 = lk[0] + lk[1]
@@ -517,8 +538,7 @@
     red_free(5)
     red_mid(0)
     red_mid(5)
-    for j in range(3):
-        c_lx(j).wait_recv()
+    landed(lx.at[0:3], I_LX)
     l2 = (lx[0] + lx[1]) + (lx[2] + lx[3])
     lt2[...] = l2
     ly[y] = l2
@@ -530,7 +550,7 @@
 
     def c_ox(t):
         m, to = plane(t)
-        return rc(ox_s.at[m], fin_b.at[mb_slot], I_OX, to)
+        return rc(ox_s.at[m], fin_b.at[mb_slot], I_OX, O_OX, to)
 
     for c in range(4):
         c_qp(3, c).wait_recv()
@@ -541,8 +561,7 @@
     for t in far_xy:
         c_ox(t).start()
     fin_b[mb_slot] = ox_s[mb_slot]
-    for j in range(3):
-        c_ly(j).wait_recv()
+    landed(ly.at[0:3], I_LY)
     l3 = (ly[0] + ly[1]) + (ly[2] + ly[3])
     lt3[...] = l3
     lz[z] = l3
@@ -551,7 +570,7 @@
 
     def c_oz(t, k_):
         s, to = pillar(t, k_)
-        return rc(oz_s.at[s, k_], fin_a.at[z, k], I_OZ, to)
+        return rc(oz_s.at[s, k_], fin_a.at[z, k], I_OZ, O_OZ, to)
 
     oz_s[0:4] = red_end(0).astype(BF)
     oz_s[4:8] = red_end(5).astype(BF)
@@ -559,8 +578,7 @@
         c_oz(t, k_).start()
     fin_a[z, k] = oz_s[z, k]
 
-    for j in range(3):
-        c_sz(j).wait_recv()
+    landed(stz.at[0:3], I_SZ)
     st = ((stz[0] + stz[1]) + (stz[2] + stz[3])) / S
     ma_, mb_ = st[0:1], st[2:3]
     inva_ = lax.rsqrt(st[1:2] - ma_ * ma_ + EPS)
@@ -568,14 +586,13 @@
     c_ = (st[4:5] - ma_ * mb_) * (inva_ * invb_)
     d_ = -2.0 * (1.0 - c_)
 
-    for j in range(7):
-        c_lz(j).wait_recv()
+    landed(lz.at[0:7], I_LZ)
     lall = lz[0]
     for i in range(1, 8):
         lall = lall + lz[i]
     loss_out[0, 0] = jnp.sum(lall[0:1, :]) / F
 
-    all_pieces(I_OX).wait_recv()
+    landed(bt_loc.at[0:15], I_OX)
     for c in range(4):
         at = slice(c * 128, (c + 1) * 128)
         an = (a_in[:, at].astype(F32) - ma_[:, at]) * inva_[:, at]
@@ -583,7 +600,7 @@
         gt = fin_b[4 * c:4 * c + 4].reshape(128, 128).astype(F32).T
         gb_out[:, at] = (invb_[:, at] * (d_[:, at] * (an - c_[:, at] * bn) + gt)).astype(BF)
 
-    all_pieces(I_OZ).wait_recv()
+    landed(bt_loc.at[0:15], I_OZ)
     for c in range(4):
         at = slice(c * 128, (c + 1) * 128)
         an = (a_in[:, at].astype(F32) - ma_[:, at]) * inva_[:, at]
@@ -591,36 +608,25 @@
         gt = fin_a[2 * c:2 * c + 2].reshape(128, 128).astype(F32).T
         ga_out[:, at] = (inva_[:, at] * (d_[:, at] * (bn - c_[:, at] * an) + gt)).astype(BF)
 
-    for c in (c_sk, c_lk):
-        c.wait_send()
-    for i in (I_V1, I_W1, I_OX, I_OZ):
-        all_pieces(i).wait_send()
-    for j in range(3):
-        for c in (c_sx, c_sz, c_lx, c_ly):
-            c(j).wait_send()
-    for j in range(7):
-        c_lz(j).wait_send()
-    for i in range(4):
-        c_gd(i).wait_send()
-    for i in range(10):
-        for c in (c_gp, c_gm, c_gpf, c_gmf, c_r1p, c_r1m):
-            c(i).wait_send()
-        for h in (0, 1):
-            c_r2p(i, h).wait_send()
-            c_r2m(i, h).wait_send()
-    for n in range(8):
-        for c in range(4):
-            c_wd(n, c).wait_send()
-    for n in range(4):
-        for c in range(4):
-            if in_p(n, c):
-                c_zp(n, c).wait_send()
-            if in_m(n, c):
-                c_zm(n, c).wait_send()
-            if in_p(3 - n, c):
-                c_qp(n, c).wait_send()
-            if in_m(3 - n, c):
-                c_qm(n, c).wait_send()
+    for e in (O_V1, O_W1, O_OX, O_OZ):
+        left(bt_loc.at[0:15], e)
+    left(st1, O_SK)
+    left(stx.at[0:3], O_SX)
+    left(stz.at[0:3], O_SZ)
+    left(lt0, O_LK)
+    left(lx.at[0:3], O_LX)
+    left(ly.at[0:3], O_LY)
+    left(lz.at[0:7], O_LZ)
+    for e in (O_GP, O_GM, O_R2P, O_R2M):
+        left(r2p_s, e)
+    for e in (O_GPF, O_GMF, O_R1P, O_R1M):
+        left(r1p_s, e)
+    for e in (O_WD, O_GD):
+        left(gd_s, e)
+    for e in (O_ZP, O_ZM, O_QP + 1, O_QM + 1):
+        left(qp_s.at[0:3], e)
+    for e in (O_ZP + 1, O_ZM + 1, O_QP, O_QM):
+        left(qp_s.at[0, 0:2], e)
 
 
 def shards(view_a, view_b):
@@ -629,13 +635,14 @@
     ga, gb, loss = pl.pallas_call(
         kernel,
         out_shape=(block, block, jax.ShapeDtypeStruct((1, 1), F32)),
-        in_specs=[pl.BlockSpec(memory_space=vm)] * 2,
+        in_specs=[pl.BlockSpec(memory_space=pltpu.HBM)] * 2,
         out_specs=(
             pl.BlockSpec(memory_space=vm),
             pl.BlockSpec(memory_space=vm),
             pl.BlockSpec(memory_space=pltpu.SMEM),
         ),
         scratch_shapes=[
+            vm((128, 512), BF), vm((128, 512), BF),
             vm((8, 2, 32, 128), BF), vm((16, 32, 128), BF),
             vm((4, 4, 2, 4, 2, 32, 128), BF),
             vm((2, 4, 2, 4, 4, 32, 128), BF),
@@ -654,8 +661,9 @@
             vm((16, 32, 128), BF), vm((16, 32, 128), BF),
             *[vm((8, 128), F32)] * 4,
             vm((2, 8, 128), F32), vm((4, 8, 128), F32), vm((4, 8, 128), F32), vm((8, 8, 128), F32),
-            pltpu.SemaphoreType.DMA((N_SEM,)),
-            pltpu.SemaphoreType.DMA((N_SEM,)),
+            pltpu.SemaphoreType.DMA((N_SEND,)),
+            pltpu.SemaphoreType.DMA((N_RECV,)),
+            pltpu.SemaphoreType.DMA((2,)),
         ],
         compiler_params=pltpu.CompilerParams(
             collective_id=0, has_side_effects=True, vmem_limit_bytes=56 * 1024 * 1024

time: 77.3 us -> 72.8 us (0.942)
  Pallas kernels: 72.6 us -> 68.1 us
    pallas_call x1, Pallas kernels: 72.6 us -> 68.1 us  [shards(): pl.pallas_call(kernel, out_shape=(block, block, jax.ShapeDtypeStruct((1,...]
where the time goes in v3:
time: 72.8 us; the launch traced here: 72.6 us
  Pallas kernels  68.1 us (94%)
  between operations  2.32 us (3%)
  local copies, waits for them, and re-layouts  2.26 us (3%)
    pallas_call x1, Pallas kernels, shards(): pl.pallas_call(kernel, out_shape=(block, block, jax.ShapeDtypeStruct((1,...  68.1 us
    unnamed x4, local copies, waits for them, and re-layouts  2.26 us

profile of v3, /device:TPU:1, one launch (start us, length us, event | category | flops | bytes accessed | tf_op | source)
XLA Modules:
  0.0 72.6 jit_solution(10004877936675754404)
XLA Ops:
  0.6 68.1 %shard_map.49 = (bf16[128,512]{1,0:T(8,128)(2,1)}, bf16[128,512]{1,0:T(8,128)(2,1)}, f32[1,1]{1,0:T(1,128)}) custom-call(bf16[128,512]{1,0:T(8,128)(2,1)} %a_hbm.1, bf16[128,512]{1,0:T(8,128)(2,1)} %b_hbm.1), custom_call_target="tpu_custom_call" | custom-call | tf_op jit(solution)/shard_map/pallas_call | solution.py:635
  68.7 0.0 copy-start
  68.7 1.6 %copy.8 = bf16[128,512]{1,0:T(8,128)(2,1)} copy(bf16[128,512]{1,0:T(8,128)(2,1)} %get-tuple-element.12) | data formatting | bytes 262144
  70.3 0.0 copy-done
  70.3 0.7 copy.9
Async XLA Ops:
  68.7 1.6 %copy-start = (bf16[128,512]{1,0:T(8,128)(2,1)S(1)}, bf16[128,512]{1,0:T(8,128)(2,1)}, u32[]{:S(2)}) copy-start(bf16[128,512]{1,0:T(8,128)(2,1)} %get-tuple-element.13) | copy-start | bytes 393220

commit v4 on v3

--- a/solution.py
+++ b/solution.py
@@ -480,32 +480,34 @@
                 qm_s[n, c] = v.astype(BF)
                 c_qm(n, c).start()
 
-    ga_strip(x2)
-    red_first(9)
-    for i in (4, 3, 2, 1):
-        red_first(i)
     gb_own(0)
     q_send(0, True)
+    ga_strip(x2)
+    for i in (9, 4, 3, 2, 1):
+        red_first(i)
     gb_own(1)
     gb_own(2)
     q_send(1, True)
-    gb_own(3)
     ga_strip(xp)
     red_first(8)
     ga_strip(xm)
     red_first(7)
-    for i in (9, 4, 8, 7, 3, 2, 1):
+    red_free(9)
+    red_free(4)
+    gb_own(3)
+    q_send(1, False)
+    red_mid(9)
+    red_mid(4)
+    for i in (8, 7, 3, 2, 1):
         red_free(i)
     ga_strip(x)
     red_first(6)
     red_free(6)
-    red_mid(9)
-    red_mid(4)
-    q_send(1, False)
-    red_mid(8)
-    red_mid(3)
-    red_mid(7)
-    red_mid(2)
+    for i in (8, 3):
+        red_mid(i)
+    q_send(2, False)
+    for i in (7, 2):
+        red_mid(i)
 
     def c_lx(j):
         return rc(lt1, lx.at[x], I_LX, O_LX, dev((xm, xp, x2)[j], y, z, k))
@@ -529,15 +531,12 @@
     red_first(5)
     red_mid(6)
     red_mid(1)
-    q_send(2, False)
     gaf[y, xp, 0] = red_end(8)
     gaf[y, xm, 0] = red_end(7)
     red_free(0)
     gaf[yp, x, 1] = red_end(3)
     gaf[ym, x, 1] = red_end(2)
     red_free(5)
-    red_mid(0)
-    red_mid(5)
     landed(lx.at[0:3], I_LX)
     l2 = (lx[0] + lx[1]) + (lx[2] + lx[3])
     lt2[...] = l2
@@ -545,12 +544,14 @@
     for j in range(3):
         c_ly(j).start()
     q_send(3, False)
+    red_mid(0)
+    red_mid(5)
     gaf[y, x, 0] = red_end(6)
     gaf[y, x, 1] = red_end(1)
 
-    def c_ox(t):
-        m, to = plane(t)
-        return rc(ox_s.at[m], fin_b.at[mb_slot], I_OX, O_OX, to)
+    def c_ox(x_, y_):
+        m = x_ * 4 + y_
+        return rc(ox_s.at[m], fin_b.at[mb_slot], I_OX, O_OX, dev(x_, y_, z, k))
 
     for c in range(4):
         c_qp(3, c).wait_recv()
@@ -558,8 +559,13 @@
         v = z_part(0, c) + qp_r[3, c].astype(F32) + qm_r[3, c].astype(F32)
         for x_ in range(4):
             ox_s[x_ * 4 + c] = v[x_].astype(BF)
-    for t in far_xy:
-        c_ox(t).start()
+        for x_ in (x2, xm, xp):
+            c_ox(x_, c).start()
+
+        @pl.when(y != c)
+        def _():
+            c_ox(x, c).start()
+
     fin_b[mb_slot] = ox_s[mb_slot]
     landed(ly.at[0:3], I_LY)
     l3 = (ly[0] + ly[1]) + (ly[2] + ly[3])
@@ -568,14 +574,21 @@
     for j in range(7):
         c_lz(j).start()
 
-    def c_oz(t, k_):
-        s, to = pillar(t, k_)
-        return rc(oz_s.at[s, k_], fin_a.at[z, k], I_OZ, O_OZ, to)
-
-    oz_s[0:4] = red_end(0).astype(BF)
-    oz_s[4:8] = red_end(5).astype(BF)
-    for t, k_ in far_z:
-        c_oz(t, k_).start()
+    def c_oz(s, k_):
+        return rc(oz_s.at[s, k_], fin_a.at[z, k], I_OZ, O_OZ, dev(x, y, s, k_))
+
+    for h, i in ((0, 0), (1, 5)):
+        oz_s[4 * h:4 * h + 4] = red_end(i).astype(BF)
+        for d in (2, 3, 1, 0):
+            s = 4 * h + lax.rem(zl + d, 4)
+            c_oz(s, o).start()
+            if d:
+                c_oz(s, k).start()
+            else:
+                @pl.when(zh != h)
+                def _():
+                    c_oz(s, k).start()
+
     fin_a[z, k] = oz_s[z, k]
 
     landed(stz.at[0:3], I_SZ)

time: 72.8 us -> 69.2 us (0.951)
  Pallas kernels: 68.1 us -> 64.5 us
    pallas_call x1, Pallas kernels: 68.1 us -> 64.5 us  [shards(): pl.pallas_call(kernel, out_shape=(block, block, jax.ShapeDtypeStruct((1,...]
where the time goes in v4:
time: 69.2 us; the launch traced here: 69 us
  Pallas kernels  64.5 us (93%)
  between operations  2.32 us (3%)
  local copies, waits for them, and re-layouts  2.26 us (3%)
    pallas_call x1, Pallas kernels, shards(): pl.pallas_call(kernel, out_shape=(block, block, jax.ShapeDtypeStruct((1,...  64.5 us
    unnamed x4, local copies, waits for them, and re-layouts  2.26 us

profile of v4, /device:TPU:1, one launch (start us, length us, event | category | flops | bytes accessed | tf_op | source)
XLA Modules:
  0.0 69.0 jit_solution(5384600066332813323)
XLA Ops:
  0.6 64.5 %shard_map.49 = (bf16[128,512]{1,0:T(8,128)(2,1)}, bf16[128,512]{1,0:T(8,128)(2,1)}, f32[1,1]{1,0:T(1,128)}) custom-call(bf16[128,512]{1,0:T(8,128)(2,1)} %a_hbm.1, bf16[128,512]{1,0:T(8,128)(2,1)} %b_hbm.1), custom_call_target="tpu_custom_call" | custom-call | tf_op jit(solution)/shard_map/pallas_call | solution.py:648
  65.1 0.0 copy-start
  65.1 1.6 %copy.8 = bf16[128,512]{1,0:T(8,128)(2,1)} copy(bf16[128,512]{1,0:T(8,128)(2,1)} %get-tuple-element.12) | data formatting | bytes 262144
  66.7 0.0 copy-done
  66.7 0.7 copy.9
Async XLA Ops:
  65.1 1.6 %copy-start = (bf16[128,512]{1,0:T(8,128)(2,1)S(1)}, bf16[128,512]{1,0:T(8,128)(2,1)}, u32[]{:S(2)}) copy-start(bf16[128,512]{1,0:T(8,128)(2,1)} %get-tuple-element.13) | copy-start | bytes 393220
